TPU v7x, 128 devices: a whole 4x4x4 slice. The times are simulated.
128 devices in a mesh: branch: 4 (over z_lo, core), query: 32 (over z_hi, x, y).
Axes of the slice: x: 4, y: 4, z: 4 (z_hi: 2, z_lo: 2; z = z_hi * 2 + z_lo), core: 2. Of those that a mesh axis runs over, the one named last changes fastest.
Arguments:
- sensors: bfloat16 [3, 128, 2048], P(None, ('branch', 'query')), may hold values from -24 to 24
- branch_w: bfloat16 [3, 2048, 1024], replicated, may hold values from -0.125 to 0.125
- branch_b: float32 [3, 1024], replicated, may hold values from -3 to 3
- coords: bfloat16 [3, 65536], P(None, ('branch', 'query')), may hold values from -1 to 1
- func_index: int32 [65536], P(('branch', 'query')), may hold values from 0 to 31
- targets: float32 [65536], P(('branch', 'query')), may hold values from -6 to 6
- trunk_w1: bfloat16 [3, 1024], replicated, may hold values from -3.5 to 3.5
- trunk_b1: float32 [1024], replicated, may hold values from -3 to 3
- trunk_w2: bfloat16 [1024, 1024], replicated, may hold values from -0.1875 to 0.1875
- trunk_b2: float32 [1024], replicated, may hold values from -3 to 3
Outputs:
- grad_branch_w: float32 [3, 2048, 1024], P(None, 'query')
- grad_branch_b: float32 [3, 1024], replicated
- grad_trunk_w1: float32 [3, 1024], replicated
- grad_trunk_b1: float32 [1024], replicated
- grad_trunk_w2: float32 [1024, 1024], replicated
- grad_trunk_b2: float32 [1024], replicated
Inputs may be any that keep to these rules, and one draw needn't show every extreme that they name: func_index[i] names one of the 32 function samples whose rows of sensors stand in the same owner group (index of the mesh axis branch) as query point i.
All inputs are finite; a program needn't handle non-finite values.
Results may differ from a plain program's by a relative error of at most 0.018.
Values may be sent and summed in bfloat16 or wider, within the bound.
A program may use at most 128 MiB of HBM per device.

v0:
```python
import jax
import jax.numpy as jnp
from jax import lax
from jax.sharding import PartitionSpec as P


def joined_along(pieces, dim):
    lengths = list(pieces.shape[1:])
    lengths[dim] *= pieces.shape[0]
    return jnp.moveaxis(pieces, 0, dim).reshape(lengths)


def from_everyone(array, axis):
    copies = jnp.broadcast_to(array, (lax.axis_size(axis), *array.shape))
    return lax.all_to_all(copies, axis, split_axis=0, concat_axis=0, tiled=True)


def gathered_copies(array, axis, dim):
    return joined_along(from_everyone(array, axis), dim)


def cut_along(array, dim, length):
    before, after = (array.shape[:dim], array.shape[dim + 1 :])
    return jnp.moveaxis(array.reshape(*before, length, -1, *after), dim, 0)


def sum_at_owner(array, axis, dim):
    length = lax.axis_size(axis)
    pieces = lax.all_to_all(cut_along(array, dim, length), axis, 0, 0, tiled=True)
    return jnp.sum(pieces, axis=0)


def side_by_side(arrays, axis, dim, along):
    both = jnp.concatenate(arrays, axis=along)
    whole, at, done = (lax.all_gather(both, axis, axis=dim, tiled=True), 0, [])
    for a in arrays:
        done.append(lax.slice_in_dim(whole, at, at + a.shape[along], axis=along))
        at += a.shape[along]
    return tuple(done)


def shards(
    sensors, branch_w, branch_b, coords, func_index, targets, trunk_w1, trunk_b1, trunk_w2, trunk_b2
):
    branches, func_dev, sensor_count = sensors.shape
    width = branch_w.shape[2]
    scale = width ** (-0.5)
    total_funcs = func_dev * lax.axis_size("branch") * lax.axis_size("query")
    pre = (
        jnp.einsum("kfs,ksl->kfl", sensors, branch_w, preferred_element_type=jnp.float32)
        + branch_b[:, None, :]
    )
    latent = jnp.tanh(pre).astype(jnp.bfloat16)
    lat_full = latent.astype(jnp.float32)
    every = gathered_copies(latent, "query", 1).astype(jnp.float32)
    product = (every[0] * every[1] * every[2]).astype(jnp.bfloat16)
    group_funcs = product.shape[0]
    onehot = (func_index[:, None] == jnp.arange(group_funcs, dtype=jnp.int32)[None, :]).astype(
        jnp.bfloat16
    )
    first = lax.dot_general(
        coords, trunk_w1, (((0,), (0,)), ((), ())), preferred_element_type=jnp.float32
    )
    hidden = jnp.tanh(first + trunk_b1).astype(jnp.bfloat16)
    trunk_out = jnp.dot(hidden, trunk_w2, preferred_element_type=jnp.float32) + trunk_b2
    picked = jnp.dot(onehot, product, preferred_element_type=jnp.float32)
    pred = jnp.sum(picked * trunk_out, axis=1) * scale
    resid = (pred - targets) / total_funcs
    weighted = (resid[:, None] * trunk_out * scale).astype(jnp.bfloat16)
    dprod = sum_at_owner(
        lax.dot_general(
            onehot, weighted, (((0,), (0,)), ((), ())), preferred_element_type=jnp.float32
        ),
        "query",
        0,
    )
    grad_out = (resid[:, None] * picked * scale).astype(jnp.bfloat16)
    gw2 = lax.dot_general(
        hidden, grad_out, (((0,), (0,)), ((), ())), preferred_element_type=jnp.float32
    )
    gb2 = jnp.sum(grad_out.astype(jnp.float32), axis=0)
    grad_hidden = lax.dot_general(
        grad_out, trunk_w2, (((1,), (1,)), ((), ())), preferred_element_type=jnp.float32
    )
    hid_full = hidden.astype(jnp.float32)
    grad_pre = (grad_hidden * (1.0 - hid_full * hid_full)).astype(jnp.bfloat16)
    gw1 = lax.dot_general(
        coords, grad_pre, (((1,), (0,)), ((), ())), preferred_element_type=jnp.float32
    )
    gb1 = jnp.sum(grad_pre.astype(jnp.float32), axis=0)
    others = jnp.stack(
        [lat_full[1] * lat_full[2], lat_full[0] * lat_full[2], lat_full[0] * lat_full[1]]
    )
    delta = (dprod[None] * others * (1.0 - lat_full * lat_full)).astype(jnp.bfloat16)
    row_count = sensor_count // lax.axis_size("query")
    first_row = lax.axis_index("query") * row_count
    piece_sensors, piece_delta = side_by_side((sensors, delta), ("branch", "query"), 1, 2)
    cut = lax.dynamic_slice_in_dim(piece_sensors, first_row, row_count, 2)
    grad_branch_w = jnp.einsum("kfs,kfl->ksl", cut, piece_delta, preferred_element_type=jnp.float32)
    gbb = jnp.sum(delta.astype(jnp.float32), axis=1)
    gbb, gw1, gb1, gw2, gb2 = lax.psum((gbb, gw1, gb1, gw2, gb2), ("branch", "query"))
    return (grad_branch_w, gbb, gw1, gb1, gw2, gb2)


def solution(mesh):
    placed = (
        P(None, ("branch", "query"), None),
        P(),
        P(),
        P(None, ("branch", "query")),
        P(("branch", "query")),
        P(("branch", "query")),
        P(),
        P(),
        P(),
        P(),
    )
    return jax.shard_map(
        shards,
        mesh=mesh,
        in_specs=placed,
        out_specs=(P(None, "query", None), P(), P(), P(), P(), P()),
        check_vma=False,
    )
```

profile of v0, /device:TPU:1, one launch (start us, length us, event | category | flops | bytes accessed | tf_op | source)
XLA Modules:
  0.0 526.3 jit_solution(5017587836930844004)
XLA Ops:
  7.2 0.0 copy-start
  7.2 0.0 copy-start.4
  7.2 0.0 copy-start.7
  7.2 0.0 copy-start.9
  7.2 0.0 copy-start.10
  7.2 6.5 %fusion.11 = f32[3,1,1024]{2,1,0:T(1,128)S(1)} fusion(bf16[3,2048,1024]{2,1,0:T(8,128)(2,1)} %param.11, bf16[3,2048,1]{1,0,2:T(4,128)(2,1)} %bitcast.33), kind=kOutput, calls=%fused_computation.24 | convolution fusion | flops 12582912 | bytes 12607488 | tf_op jit(solution)/shard_map/kfs,ksl->kfl/dot_general | solution.py:50
  13.7 0.0 copy-done.4
  13.7 0.8 broadcast_in_dim.2
  14.5 11.2 %all-to-all-start = ((bf16[32,3,1,1024]{3,1,2,0:T(4,128)(2,1)}), bf16[32,3,1,1024]{3,1,2,0:T(4,128)(2,1)S(1)}, u32[]{:S(2)}, u32[]{:S(2)}) async-start(bf16[32,3,1,1024]{3,1,2,0:T(4,128)(2,1)} %broadcast_in_dim.2), calls=%async_computation | async-start | bytes 524288 | tf_op jit(solution)/shard_map/all_to_all | solution.py:15
  25.7 0.0 copy-done.7
  25.7 0.0 copy-done.9
  25.7 0.0 copy-done.10
  25.7 0.5 tanh_convert_fusion
  26.2 0.0 copy-start.2
  26.2 1.0 copy-done.2
  27.2 0.0 copy-done
  27.2 2.6 fusion.20
  29.8 5.3 %all-to-all-done = bf16[32,3,1,1024]{3,1,2,0:T(4,128)(2,1)S(1)} async-done(((bf16[32,3,1,1024]{3,1,2,0:T(4,128)(2,1)}), bf16[32,3,1,1024]{3,1,2,0:T(4,128)(2,1)S(1)}, u32[]{:S(2)}, u32[]{:S(2)}) %all-to-all-start) | async-done | bytes 196640 | tf_op jit(solution)/shard_map/all_to_all | solution.py:15
  35.1 0.1 convert_bitcast_fusion
  35.2 0.0 copy-done.5
  35.2 0.0 copy-done.6
  35.2 0.0 copy-start.8
  35.3 0.0 copy-start.1
  35.3 3.6 multiply_reduce_fusion
  38.8 0.0 copy-done.8
  38.8 0.0 copy-done.1
  38.8 0.5 convolution_bitcast_fusion
  39.4 0.8 copy.26
  40.2 4.0 all-to-all-start.1
  44.2 0.0 all-gather.2.cloned.1.call-start
  44.2 8.9 %all-to-all-done.1 = f32[32,1,1024]{2,1,0:T(1,128)S(1)} async-done(((f32[32,1,1024]{2,1,0:T(1,128)}), f32[32,1,1024]{2,1,0:T(1,128)S(1)}, u32[]{:S(2)}, u32[]{:S(2)}) %all-to-all-start.1) | async-done | bytes 131104 | tf_op jit(solution)/shard_map/all_to_all | solution.py:29
  53.1 0.1 reduce_sum.41
  53.2 0.6 pad_maximum_fusion
  53.8 0.0 all-gather.2.cloned.1.call-update
  53.9 0.0 all-reduce.3.cloned.1.call-start
  53.9 1.9 convert_reduce_fusion
  55.8 4.5 fusion.21
  60.4 0.0 all-reduce.3.cloned.1.call-update
  60.4 2.6 convert_reduce_fusion.1
  63.0 0.2 convolution_bitcast_fusion.1
  63.2 64.8 %all-reduce = (f32[3,1024]{1,0:T(4,128)}, f32[3,1024]{1,0:T(4,128)}, f32[1024]{0:T(1024)}, f32[1024]{0:T(1024)}) all-reduce(bf16[3,1024]{1,0:T(4,128)(2,1)S(1)} %fusion.14, f32[3,1024]{1,0:T(4,128)S(1)} %convolution_bitcast_fusion.1, f32[1024]{0:T(1024)S(1)} %get-tuple-element.19, ...), channel_id=1, replica_groups=mesh['branch'=4,'query'=32] {'branch','query'}, use_global_device_ids=true, to_apply=%region_2.0 | all-reduce | flops 8192 | bytes 59392 | tf_op jit(solution)/shard_map/psum | solution.py:101
  128.1 226.8 %all-gather.2.cloned.1.call-done = bf16[3,128,3072]{2,0,1:T(4,128)(2,1)} async-done(((bf16[3,1,3072]{2,0,1:T(4,128)(2,1)}), bf16[3,128,3072]{2,0,1:T(4,128)(2,1)}) %all-gather.2.cloned.1.call-update) | async-done | bytes 2359312 | tf_op jit(solution)/shard_map/all_gather | solution.py:35
  354.9 1.6 slice-done.1
  356.5 0.1 constant_dynamic-slice_fusion
  356.6 0.1 slice-done
  356.7 1.5 fusion.2
  358.2 156.4 %all-reduce.3.cloned.1.call-done = f32[1024,1024]{1,0:T(8,128)} async-done(((f32[1024,1024]{1,0:T(8,128)}), f32[1024,1024]{1,0:T(8,128)}) %all-reduce.3.cloned.1.call-update) | async-done | bytes 4194320 | tf_op jit(solution)/shard_map/psum | solution.py:101
  514.7 4.8 copy.44
  (11 shorter events, 0.1 us)
Async XLA Ops:
  7.2 20.1 %copy-start = (bf16[1024,1024]{1,0:T(8,128)(2,1)S(1)}, bf16[1024,1024]{1,0:T(8,128)(2,1)}, u32[]{:S(2)}) copy-start(bf16[1024,1024]{1,0:T(8,128)(2,1)} %param.18) | copy-start | bytes 6291460
  7.2 6.5 %copy-start.4 = (f32[3,1024]{1,0:T(4,128)S(1)}, f32[3,1024]{1,0:T(4,128)}, u32[]{:S(2)}) copy-start(f32[3,1024]{1,0:T(4,128)} %param.12) | copy-start | bytes 36868
  7.2 18.5 %copy-start.7 = (bf16[3,512]{1,0:T(4,128)(2,1)S(1)}, bf16[3,512]{1,0:T(4,128)(2,1)}, u32[]{:S(2)}) copy-start(bf16[3,512]{1,0:T(4,128)(2,1)} %param.13) | copy-start | bytes 9220
  7.2 18.5 %copy-start.9 = (bf16[3,1024]{1,0:T(4,128)(2,1)S(1)}, bf16[3,1024]{1,0:T(4,128)(2,1)}, u32[]{:S(2)}) copy-start(bf16[3,1024]{1,0:T(4,128)(2,1)} %param.16) | copy-start | bytes 18436
  7.2 18.5 %copy-start.10 = (f32[1024]{0:T(1024)S(1)}, f32[1024]{0:T(1024)}, u32[]{:S(2)}) copy-start(f32[1024]{0:T(1024)} %param.17) | copy-start | bytes 12292
  14.5 20.6 %all-to-all-start = ((bf16[32,3,1,1024]{3,1,2,0:T(4,128)(2,1)}), bf16[32,3,1,1024]{3,1,2,0:T(4,128)(2,1)S(1)}, u32[]{:S(2)}, u32[]{:S(2)}) async-start(bf16[32,3,1,1024]{3,1,2,0:T(4,128)(2,1)} %broadcast_in_dim.2), calls=%async_computation | async-start | bytes 524288 | tf_op jit(solution)/shard_map/all_to_all | solution.py:15
  26.2 1.0 copy-start.2
  27.2 8.0 %copy-start.5 = (f32[1024]{0:T(1024)S(1)}, f32[1024]{0:T(1024)}, u32[]{:S(2)}) copy-start(f32[1024]{0:T(1024)} %param.19) | copy-start | bytes 12292
  27.2 8.0 %copy-start.6 = (s32[512]{0:T(512)S(1)}, s32[512]{0:T(512)}, u32[]{:S(2)}) copy-start(s32[512]{0:T(512)} %param.14) | copy-start | bytes 6148
  35.2 3.6 copy-start.8
  35.3 3.6 copy-start.1
  38.8 14.4 %copy-start.3 = (bf16[3,1,2048]{2,0,1:T(4,128)(2,1)S(1)}, bf16[3,1,2048]{2,0,1:T(4,128)(2,1)}, u32[]{:S(2)}) copy-start(bf16[3,1,2048]{2,0,1:T(4,128)(2,1)} %param.10) | copy-start | bytes 36868
  40.2 12.9 %all-to-all-start.1 = ((f32[32,1,1024]{2,1,0:T(1,128)}), f32[32,1,1024]{2,1,0:T(1,128)S(1)}, u32[]{:S(2)}, u32[]{:S(2)}) async-start(f32[32,1,1024]{2,1,0:T(1,128)} %copy.26), calls=%async_computation.1 | async-start | bytes 262144 | tf_op jit(solution)/shard_map/all_to_all | solution.py:29
  44.2 310.7 %all-gather.2.cloned.1.call-start = ((), (), s32[]{:S(2)}) async-start(), calls=%async_computation.2 | async-start | bytes 3170304 | tf_op jit(solution)/shard_map/all_gather | solution.py:35
  53.9 460.8 %all-reduce.3.cloned.1.call-start = ((), (), s32[]{:S(2)}) async-start(), calls=%async_computation.3 | async-start | bytes 8388608 | tf_op jit(solution)/shard_map/psum | solution.py:101
  354.9 1.6 slice-start.1
  354.9 1.9 slice-start
Sparse Core Ops, SparseCore 0:
  54.0 300.8 all-gather.1
  360.4 154.2 all-reduce.2
where the time goes:
time: 527 us; the launch traced here: 526 us
  waiting for transfers between devices  397 us (75%)
  blocking collectives  64.8 us (12%)
  matrix products  22.5 us (4%)
  starting transfers between devices  15.2 us (3%)
  between operations  14.3 us (3%)
  local copies, waits for them, and re-layouts  9.26 us (2%)
    all_gather x1, waiting for transfers between devices, side_by_side(): whole, at, done = (lax.all_gather(both, axis, axis=dim, tiled=True), 0, [])  227 us
    psum x1, waiting for transfers between devices, shards(): lax.psum((gbb, gw1, gb1, gw2, gb2), ('branch', 'query'))  156 us
    psum x1, blocking collectives, shards(): lax.psum((gbb, gw1, gb1, gw2, gb2), ('branch', 'query'))  64.8 us
    all_to_all x1, starting transfers between devices, from_everyone(): return lax.all_to_all(copies, axis, split_axis=0, concat_axis=0, tiled=True)  11.2 us
  transfers between devices with their start and end apart: 4, of which 4 were waited for; matrix products, arithmetic and copies ran while one was open for 3% of the time, Pallas kernels for 0%

commit v1 on v0

v1 whole, which is shorter than its diff:
```python
import functools

import jax
import jax.numpy as jnp
from jax import lax
from jax.experimental import pallas as pl
from jax.experimental.pallas import tpu as pltpu
from jax.sharding import PartitionSpec as P

F32 = jnp.float32
BF16 = jnp.bfloat16
ROWS = 12
CHUNKS = 4
VMEM = pltpu.VMEM


def nt(a, b):
    return lax.dot_general(a, b, (((1,), (1,)), ((), ())), preferred_element_type=F32)


def tn(a, b):
    return lax.dot_general(a, b, (((0,), (0,)), ((), ())), preferred_element_type=F32)


def nn(a, b):
    return lax.dot_general(a, b, (((1,), (0,)), ((), ())), preferred_element_type=F32)


def split(x):
    high = x.astype(BF16)
    return high, (x - high.astype(F32)).astype(BF16)


def exchange_kernel(
    sens, bw, bb, coords, fidx, targ, w1, b1, w2, b2,
    hm_out, p_out, d_out, sg_out, s_out, g_out,
    wbuf, w2buf, row8, prodsend, prodbuf, pf, latbuf, lf, sensend, sgbuf, sgf,
    hid, omh, msgf, msg, rsbuf, agbuf, hf,
    wsem, w2sem, psend, precv, lsend, lrecv, ssend, srecv, rsend, rrecv, asend, arecv,
    dsend, drecv,
):
    branch = lax.axis_index("branch")
    q = lax.axis_index("query")
    core = lax.rem(branch, 2)
    zlo = lax.div(branch, 2)
    zhi, xy = lax.div(q, 16), lax.rem(q, 16)
    x, y = lax.div(xy, 4), lax.rem(xy, 4)
    scale = 1.0 / 32.0
    rows = bw.shape[1] // CHUNKS

    def peer(d):
        dl, dq = lax.div(d, 32), lax.rem(d, 32)
        dh, dx, dy = lax.div(dq, 16), lax.rem(lax.div(dq, 4), 4), lax.rem(dq, 4)
        pz = lax.rem(zlo + dl, 2)
        pq = lax.rem(zhi + dh, 2) * 16 + lax.rem(x + dx, 4) * 4 + lax.rem(y + dy, 4)
        return pz * 2 + core, pq

    partner = (zlo * 2 + (1 - core), q)
    mine = core * 64 + zlo * 32 + q

    def wcopy(k, c):
        part = pl.ds(c * rows, rows)
        return pltpu.make_async_copy(bw.at[k, part], wbuf.at[k, part], wsem.at[k, c])

    for k in range(3):
        for c in range(CHUNKS):
            wcopy(k, c).start()
    w2copy = pltpu.make_async_copy(w2, w2buf, w2sem)
    w2copy.start()

    barrier = pltpu.get_barrier_semaphore()

    def greet(i, carry):
        pl.semaphore_signal(barrier, inc=1, device_id=peer(i), device_id_type=pl.DeviceIdType.MESH)
        return carry

    lax.fori_loop(1, 64, greet, 0)
    pl.semaphore_signal(barrier, inc=1, device_id=partner, device_id_type=pl.DeviceIdType.MESH)

    def to_peers(lo, hi, source, target, send, recv):
        def one(i, carry):
            d = hi - 1 - i
            device = peer(d)
            pltpu.make_async_remote_copy(
                src_ref=source(device), dst_ref=target(device), send_sem=send, recv_sem=recv,
                device_id=device, device_id_type=pl.DeviceIdType.MESH,
            ).start()
            return carry

        lax.fori_loop(0, hi - lo, one, 0)

    def wait(ref, sem):
        pltpu.make_async_copy(ref, ref, sem).wait()

    def swap(buf, i):
        half = buf.at[pl.ds(core * 64, 64)]
        return pltpu.make_async_remote_copy(
            src_ref=half, dst_ref=half, send_sem=dsend.at[i], recv_sem=drecv.at[i],
            device_id=partner, device_id_type=pl.DeviceIdType.MESH,
        )

    for k in range(3):
        sk = sens[k].astype(F32)
        for j in range(16):
            sgf[4 * j + k : 4 * j + k + 1, :] = sk[:, 128 * j : 128 * (j + 1)]
    for j in range(16):
        sensend[j] = sgf[4 * j : 4 * j + 4, :].astype(BF16)

    lats = []
    for k in range(3):
        pre = bb[k : k + 1, :]
        for c in range(CHUNKS):
            wcopy(k, c).wait()
            pre = pre + nn(sens[k][:, c * rows : (c + 1) * rows], wbuf[k, c * rows : (c + 1) * rows, :])
        lat = jnp.tanh(pre).astype(BF16).astype(F32)
        lats.append(lat)
        for j in range(8):
            row8[k, j : j + 1, :] = lat[:, 128 * j : 128 * (j + 1)]
        latbuf[mine, k] = row8[k].astype(BF16)
    own = (row8[0] * row8[1] * row8[2]).astype(BF16)
    prodsend[...] = own
    prodbuf[q] = own

    pl.semaphore_wait(barrier, 64)

    to_peers(1, 32, lambda d: prodsend, lambda d: prodbuf.at[q], psend, precv)
    to_peers(1, 64, lambda d: latbuf.at[mine], lambda d: latbuf.at[mine], lsend, lrecv)
    to_peers(1, 64, lambda d: sensend.at[lax.div(d[1], 2)], lambda d: sgbuf.at[mine], ssend, srecv)
    sgbuf[mine] = sensend[lax.div(q, 2)]

    for r in range(4):
        part = slice(128 * r, 128 * (r + 1))
        h = jnp.tanh(tn(coords[:, part], w1[...]) + b1[...]).astype(BF16)
        hid[part, :] = h
        hw = h.astype(F32)
        omh[part, :] = (1.0 - hw * hw).astype(BF16)

    owned = lax.broadcasted_iota(jnp.int32, (32, 512), 0) == fidx[...]

    w2copy.wait()
    wait(prodbuf.at[pl.ds(0, 31)], precv)
    for f in range(32):
        pf[8 * f : 8 * f + 8, :] = prodbuf[f].astype(F32)
    prod = jnp.concatenate([pf[pl.ds(j, 32, stride=8), :] for j in range(8)], axis=1)
    shift = jnp.sum(prod * b2[...], axis=1, keepdims=True)
    quad = nt(prod.astype(BF16), w2buf[...])
    qh, ql = split(quad)
    dots = nt(jnp.concatenate([qh, ql], axis=0), hid[...])
    dots = dots[:32] + dots[32:] + shift
    pred = jnp.sum(jnp.where(owned, dots, 0.0), axis=0, keepdims=True) * scale
    resid = (pred - targ[...]) * (1.0 / 128.0)
    a = jnp.where(owned, resid * scale, 0.0)
    ah, al = split(a)
    hsum = nn(jnp.concatenate([ah, al], axis=0), hid[...])
    hsum = hsum[:32] + hsum[32:]
    asum = jnp.sum(a, axis=1, keepdims=True)
    cf = coords[...].astype(F32)
    za = jnp.concatenate([a * cf[c : c + 1, :] for c in range(3)] + [a], axis=0).astype(BF16)
    z = nn(za, omh[...])
    gw1 = [jnp.sum(quad * z[32 * c : 32 * c + 32, :], axis=0, keepdims=True) for c in range(4)]
    for j in range(8):
        msgf[pl.ds(j, 32, stride=16), :] = hsum[:, 128 * j : 128 * (j + 1)]
        for c in range(4):
            at = 16 * (8 * c + j) + 8
            msgf[at : at + 1, :] = gw1[c][:, 128 * j : 128 * (j + 1)]
    sh, sl = split(asum)
    msgf[pl.ds(9, 32, stride=16), :] = jnp.broadcast_to(sh.astype(F32), (32, 128))
    msgf[pl.ds(10, 32, stride=16), :] = jnp.broadcast_to(sl.astype(F32), (32, 128))
    msgf[pl.ds(11, 32, stride=16), :] = jnp.zeros((32, 128), F32)
    for f in range(32):
        msg[f] = msgf[16 * f : 16 * f + ROWS, :].astype(BF16)

    to_peers(1, 32, lambda d: msg.at[d[1]], lambda d: rsbuf.at[q], rsend, rrecv)
    rsbuf[q] = msg[q]

    wait(latbuf.at[pl.ds(0, 63)], lrecv)
    wait(sgbuf.at[pl.ds(0, 63)], srecv)
    swap_lat, swap_sens = swap(latbuf, 0), swap(sgbuf, 1)
    swap_lat.start()
    swap_sens.start()

    wait(rsbuf.at[pl.ds(0, 31)], rrecv)
    total = rsbuf[0].astype(F32)
    for f in range(1, 32):
        total = total + rsbuf[f].astype(F32)
    hf[0:ROWS, :] = total
    s = hf[9:10, :] + hf[10:11, :]
    sh = s.astype(BF16).astype(F32)
    hf[9:10, :] = sh
    hf[10:11, :] = s - sh
    agbuf[mine] = hf[0:ROWS, :].astype(BF16)
    to_peers(1, 64, lambda d: agbuf.at[mine], lambda d: agbuf.at[mine], asend, arecv)

    swap_lat.wait()
    swap_sens.wait()

    def spread(i, carry):
        at = pl.multiple_of(i * 8, 8)
        for k in range(3):
            lf[k, pl.ds(at, 8), :] = latbuf[i, k].astype(F32)
        return carry

    lax.fori_loop(0, 128, spread, 0, unroll=4)

    def spread_sens(i, carry):
        sgf[pl.ds(i * 4, 4), :] = sgbuf[i].astype(F32)
        return carry

    lax.fori_loop(0, 128, spread_sens, 0, unroll=4)
    odd = lax.rem(q, 2) == 1
    for k in range(3):
        cols = sgf[pl.ds(k, 128, stride=4), :]
        sg_out[k] = jnp.where(odd, pltpu.roll(cols, 64, 1), cols).astype(BF16)
    for j in range(8):
        l0, l1, l2 = [lf[k, pl.ds(j, 128, stride=8), :] for k in range(3)]
        cols = slice(128 * j, 128 * (j + 1))
        m12, m02, m01 = l1 * l2, l0 * l2, l0 * l1
        p_out[:, cols] = (m01 * l2).astype(BF16)
        d_out[0, :, cols] = m12 * (1.0 - l0 * l0)
        d_out[1, :, cols] = m02 * (1.0 - l1 * l1)
        d_out[2, :, cols] = m01 * (1.0 - l2 * l2)

    wait(agbuf.at[pl.ds(0, 63)], arecv)
    swap_h = swap(agbuf, 2)
    swap_h.start()
    wait(prodbuf.at[pl.ds(0, 31)], psend)
    wait(latbuf.at[pl.ds(0, 63)], lsend)
    wait(sgbuf.at[pl.ds(0, 63)], ssend)
    wait(rsbuf.at[pl.ds(0, 31)], rsend)
    wait(agbuf.at[pl.ds(0, 63)], asend)
    swap_h.wait()

    def spread_h(i, carry):
        at = pl.multiple_of(i * 16, 16)
        hf[pl.ds(at, ROWS), :] = agbuf[i].astype(F32)
        return carry

    lax.fori_loop(0, 128, spread_h, 0, unroll=4)
    for j in range(8):
        hm_out[:, 128 * j : 128 * (j + 1)] = hf[pl.ds(j, 128, stride=16), :].astype(BF16)
    s_out[...] = hf[pl.ds(9, 128, stride=16), :] + hf[pl.ds(10, 128, stride=16), :]
    g = hf[pl.ds(8, 128, stride=16), :]
    g_out[...] = (g[0:32] + g[32:64]) + (g[64:96] + g[96:128])


def output_kernel(
    hm, prod, d, sg, s, g, w2, b2,
    gbw_out, gbb_out, gw1_out, gb1_out, gw2_out, gb2_out, gw2buf, sem,
):
    def drain(c):
        part = pl.ds(256 * c, 256)
        return pltpu.make_async_copy(gw2buf.at[part], gw2_out.at[part], sem.at[c])

    for c in range(4):
        gw2buf[256 * c : 256 * (c + 1), :] = tn(hm[:, 256 * c : 256 * (c + 1)], prod[...])
        drain(c).start()
    sums = s[:, 0:1]
    gp = nn(hm[...], w2[...]) + sums * b2[...]
    for k in range(3):
        delta = (gp * d[k]).astype(BF16)
        gbw_out[k] = tn(sg[k], delta)[0:64, :]
        gbb_out[k : k + 1, :] = jnp.sum(delta.astype(F32), axis=0, keepdims=True)
    gb2_out[...] = jnp.sum(sums * prod[...].astype(F32), axis=0, keepdims=True)
    for j in range(8):
        cols = slice(128 * j, 128 * (j + 1))
        for c in range(3):
            gw1_out[c : c + 1, cols] = g[8 * c + j : 8 * c + j + 1, :]
        gb1_out[:, cols] = g[24 + j : 25 + j, :]
    for c in range(4):
        drain(c).wait()


def shards(sensors, branch_w, branch_b, coords, func_index, targets, trunk_w1, trunk_b1, trunk_w2, trunk_b2):
    vmem = pl.BlockSpec(memory_space=pltpu.VMEM)
    hbm = pl.BlockSpec(memory_space=pl.ANY)
    b2 = trunk_b2.reshape(1, 1024)
    shape = jax.ShapeDtypeStruct
    dma = pltpu.SemaphoreType.DMA
    hm, prod, d, sg, s, g = pl.pallas_call(
        exchange_kernel,
        out_shape=(
            shape((128, 1024), BF16), shape((128, 1024), BF16), shape((3, 128, 1024), F32),
            shape((3, 128, 128), BF16), shape((128, 128), F32), shape((32, 128), F32),
        ),
        in_specs=[vmem, hbm, vmem, vmem, vmem, vmem, vmem, vmem, hbm, vmem],
        out_specs=(vmem,) * 6,
        scratch_shapes=[
            VMEM((3, 2048, 1024), BF16), VMEM((1024, 1024), BF16), VMEM((3, 8, 128), F32),
            VMEM((8, 128), BF16), VMEM((32, 8, 128), BF16), VMEM((256, 128), F32),
            VMEM((128, 3, 8, 128), BF16), VMEM((3, 1024, 128), F32),
            VMEM((16, 4, 128), BF16), VMEM((128, 4, 128), BF16), VMEM((512, 128), F32),
            VMEM((512, 1024), BF16), VMEM((512, 1024), BF16),
            VMEM((512, 128), F32), VMEM((32, ROWS, 128), BF16), VMEM((32, ROWS, 128), BF16),
            VMEM((128, ROWS, 128), BF16), VMEM((2048, 128), F32),
            dma((3, CHUNKS)), dma, dma, dma, dma, dma, dma, dma, dma, dma, dma, dma,
            dma((3,)), dma((3,)),
        ],
        compiler_params=pltpu.CompilerParams(
            collective_id=0, has_side_effects=True, vmem_limit_bytes=40 * 1024 * 1024
        ),
        name="exchange",
    )(
        sensors, branch_w, branch_b, coords, func_index.reshape(1, 512), targets.reshape(1, 512),
        trunk_w1, trunk_b1.reshape(1, 1024), trunk_w2, b2,
    )
    gbw, gbb, gw1, gb1, gw2, gb2 = pl.pallas_call(
        output_kernel,
        out_shape=(
            shape((3, 64, 1024), F32), shape((3, 1024), F32), shape((3, 1024), F32),
            shape((1, 1024), F32), shape((1024, 1024), F32), shape((1, 1024), F32),
        ),
        in_specs=[vmem] * 8,
        out_specs=(vmem, vmem, vmem, vmem, hbm, vmem),
        scratch_shapes=[VMEM((1024, 1024), F32), dma((4,))],
        compiler_params=pltpu.CompilerParams(vmem_limit_bytes=32 * 1024 * 1024),
        name="outputs",
    )(hm, prod, d, sg, s, g, trunk_w2, b2)
    return gbw, gbb, gw1, gb1.reshape(1024), gw2, gb2.reshape(1024)


def solution(mesh):
    both = ("branch", "query")
    placed = (P(None, both, None), P(), P(), P(None, both), P(both), P(both), P(), P(), P(), P())
    return jax.shard_map(
        shards,
        mesh=mesh,
        in_specs=placed,
        out_specs=(P(None, "query", None), P(), P(), P(), P(), P()),
        check_vma=False,
    )
```

time: 527 us -> 45.5 us (0.09)
  waiting for transfers between devices: 397 us -> 0 us
  blocking collectives: 64.8 us -> 0 us
  Pallas kernels: 0 us -> 37.2 us
  matrix products: 22.5 us -> 0 us
  starting transfers between devices: 15.2 us -> 0 us
  between operations: 14.3 us -> 0.66 us
    all_gather x1 -> x0, waiting for transfers between devices: 227 us -> none  [side_by_side(): whole, at, done = (lax.all_gather(both, axis, axis=dim, tiled=True), 0, [])]
    psum x1 -> x0, waiting for transfers between devices: 156 us -> none  [shards(): lax.psum((gbb, gw1, gb1, gw2, gb2), ('branch', 'query'))]
    psum x1 -> x0, blocking collectives: 64.8 us -> none  [shards(): lax.psum((gbb, gw1, gb1, gw2, gb2), ('branch', 'query'))]
    pallas_call x0 -> x2, Pallas kernels: none -> 37.2 us  [the longest x1 33.9 us: shards(): pl.pallas_call(exchange_kernel, out_shape=(shape((128, 1024), BF16), shap...]
    dot_general x9 -> x0, matrix products: 22.5 us -> none  [the longest x1 6.46 us: shards(): jnp.einsum('kfs,ksl->kfl', sensors, branch_w, preferred_element_type=jnp....]
    all_to_all x2 -> x0, starting transfers between devices: 15.1 us -> none  [the longest x1 11.2 us: from_everyone(): return lax.all_to_all(copies, axis, split_axis=0, concat_axis=0, tiled=True)]
    all_to_all x2 -> x0, waiting for transfers between devices: 14.2 us -> none  [the longest x1 8.85 us: sum_at_owner(): lax.all_to_all(cut_along(array, dim, length), axis, 0, 0, tiled=True)]
  transfers between devices with their start and end apart: 4 -> 0, of which waited for: 4 -> 0; matrix products, arithmetic and copies ran while one was open for 3% -> 0% of each run, Pallas kernels for 0% -> 0%
where the time goes in v1:
time: 45.5 us; the launch traced here: 45 us
  Pallas kernels  37.2 us (82%)
  local copies, waits for them, and re-layouts  7.16 us (16%)
  between operations  0.66 us (1%)
    pallas_call x1, Pallas kernels, shards(): pl.pallas_call(exchange_kernel, out_shape=(shape((128, 1024), BF16), shap...  33.9 us
    unnamed x17, local copies, waits for them, and re-layouts  7.16 us
    pallas_call x1, Pallas kernels, shards(): pl.pallas_call(output_kernel, out_shape=(shape((3, 64, 1024), F32), shape...  3.26 us

profile of v1, /device:TPU:1, one launch (start us, length us, event | category | flops | bytes accessed | tf_op | source)
XLA Modules:
  0.0 45.0 jit_solution(4080098912254601957)
XLA Ops:
  0.6 0.7 %copy.16.sens = bf16[3,1,2048]{2,1,0:T(2,128)(2,1)S(1)} copy(bf16[3,1,2048]{2,0,1:T(4,128)(2,1)} %param.10) | data formatting | bytes 24576 | tf_op args[0]
  1.4 0.0 copy-start
  1.4 1.6 %copy-done = bf16[1024,1024]{1,0:T(8,128)(2,1)S(1)} copy-done((bf16[1024,1024]{1,0:T(8,128)(2,1)S(1)}, bf16[1024,1024]{1,0:T(8,128)(2,1)}, u32[]{:S(2)}) %copy-start) | copy-done | bytes 2097176
  3.0 0.0 copy-start.1
  3.0 0.7 %copy-done.1 = f32[3,1024]{1,0:T(4,128)S(1)} copy-done((f32[3,1024]{1,0:T(4,128)S(1)}, f32[3,1024]{1,0:T(4,128)}, u32[]{:S(2)}) %copy-start.1) | copy-done | bytes 12312
  3.7 0.0 copy-start.2
  3.7 0.7 %copy-done.2 = f32[1024]{0:T(1024)S(1)} copy-done((f32[1024]{0:T(1024)S(1)}, f32[1024]{0:T(1024)}, u32[]{:S(2)}) %copy-start.2) | copy-done | bytes 4120
  4.4 0.0 copy-start.3
  4.4 0.7 %copy-done.3 = bf16[3,1024]{1,0:T(4,128)(2,1)S(1)} copy-done((bf16[3,1024]{1,0:T(4,128)(2,1)S(1)}, bf16[3,1024]{1,0:T(4,128)(2,1)}, u32[]{:S(2)}) %copy-start.3) | copy-done | bytes 6168
  5.1 0.0 copy-start.4
  5.1 0.7 %copy-done.4 = bf16[3,512]{1,0:T(4,128)(2,1)S(1)} copy-done((bf16[3,512]{1,0:T(4,128)(2,1)S(1)}, bf16[3,512]{1,0:T(4,128)(2,1)}, u32[]{:S(2)}) %copy-start.4) | copy-done | bytes 3096
  5.8 0.0 copy-start.5
  5.8 0.7 %copy-done.5 = f32[1024]{0:T(1024)S(1)} copy-done((f32[1024]{0:T(1024)S(1)}, f32[1024]{0:T(1024)}, u32[]{:S(2)}) %copy-start.5) | copy-done | bytes 4120
  6.4 0.0 copy-start.6
  6.4 0.7 %copy-done.6 = s32[512]{0:T(512)S(1)} copy-done((s32[512]{0:T(512)S(1)}, s32[512]{0:T(512)}, u32[]{:S(2)}) %copy-start.6) | copy-done | bytes 2072
  7.1 0.0 copy-start.7
  7.1 0.7 %copy-done.7 = f32[512]{0:T(512)S(1)} copy-done((f32[512]{0:T(512)S(1)}, f32[512]{0:T(512)}, u32[]{:S(2)}) %copy-start.7) | copy-done | bytes 2072
  7.8 33.9 %exchange.1 = (bf16[128,1024]{1,0:T(8,128)(2,1)S(1)}, bf16[128,1024]{1,0:T(8,128)(2,1)S(1)}, f32[3,128,1024]{2,1,0:T(8,128)S(1)}, bf16[3,128,128]{2,1,0:T(8,128)...) custom-call(bf16[3,1,2048]{2,1,0:T(2,128)(2,1)S(1)} %copy.16.sens, bf16[3,2048,1024]{2,1,0:T(8,128)(2,1)} %bw.1, ...), custom_call_target="tpu_custom_call" | custom-call | tf_op jit(solution)/shard_map/exchange/pallas_call | solution.py:279
  41.7 3.3 %outputs.1 = (f32[3,64,1024]{2,1,0:T(8,128)}, f32[3,1024]{1,0:T(4,128)}, f32[3,1024]{1,0:T(4,128)}, f32[1,1024]{1,0:T(1,128)}, f32[1024,1024]{1,0:T(8,128)}, /*index=5*/f32[1,1024]{1,0:T(1,128)}) custom-call(bf16[128,1024]{1,0:T(8,128)(2,1)S(1)} %get-tuple-element.18.hm, bf16[128,1024]{1,0:T(8,128)(2,1)S(1)} %get-tuple-element.19.prod, ...), custom_call_target="tpu_custom_call" | custom-call | tf_op jit(solution)/shard_map/outputs/pallas_call | solution.py:306
Async XLA Ops:
  1.4 1.6 %copy-start = (bf16[1024,1024]{1,0:T(8,128)(2,1)S(1)}, bf16[1024,1024]{1,0:T(8,128)(2,1)}, u32[]{:S(2)}) copy-start(bf16[1024,1024]{1,0:T(8,128)(2,1)} %w2.3) | copy-start | bytes 6291460
  3.0 0.7 %copy-start.1 = (f32[3,1024]{1,0:T(4,128)S(1)}, f32[3,1024]{1,0:T(4,128)}, u32[]{:S(2)}) copy-start(f32[3,1024]{1,0:T(4,128)} %bb.1) | copy-start | bytes 36868
  3.7 0.7 %copy-start.2 = (f32[1024]{0:T(1024)S(1)}, f32[1024]{0:T(1024)}, u32[]{:S(2)}) copy-start(f32[1024]{0:T(1024)} %param.19) | copy-start | bytes 12292
  4.4 0.7 %copy-start.3 = (bf16[3,1024]{1,0:T(4,128)(2,1)S(1)}, bf16[3,1024]{1,0:T(4,128)(2,1)}, u32[]{:S(2)}) copy-start(bf16[3,1024]{1,0:T(4,128)(2,1)} %w1.1) | copy-start | bytes 18436
  5.1 0.7 %copy-start.4 = (bf16[3,512]{1,0:T(4,128)(2,1)S(1)}, bf16[3,512]{1,0:T(4,128)(2,1)}, u32[]{:S(2)}) copy-start(bf16[3,512]{1,0:T(4,128)(2,1)} %coords.1) | copy-start | bytes 9220
  5.8 0.7 %copy-start.5 = (f32[1024]{0:T(1024)S(1)}, f32[1024]{0:T(1024)}, u32[]{:S(2)}) copy-start(f32[1024]{0:T(1024)} %param.17) | copy-start | bytes 12292
  6.4 0.7 %copy-start.6 = (s32[512]{0:T(512)S(1)}, s32[512]{0:T(512)}, u32[]{:S(2)}) copy-start(s32[512]{0:T(512)} %param.14) | copy-start | bytes 6148
  7.1 0.7 %copy-start.7 = (f32[512]{0:T(512)S(1)}, f32[512]{0:T(512)}, u32[]{:S(2)}) copy-start(f32[512]{0:T(512)} %param.15) | copy-start | bytes 6148

commit v2 on v1

--- a/solution.py
+++ b/solution.py
@@ -1,5 +1,3 @@
-import functools
-
 import jax
 import jax.numpy as jnp
 from jax import lax
@@ -32,11 +30,12 @@
 
 
 def exchange_kernel(
-    sens, bw, bb, coords, fidx, targ, w1, b1, w2, b2,
-    hm_out, p_out, d_out, sg_out, s_out, g_out,
+    sens_hbm, bw, bb_hbm, coords_hbm, fidx_hbm, targ_hbm, w1_hbm, b1_hbm, w2, b2_hbm,
+    hm_out, p_out, delta_out, sg_out, s_out, g_out,
+    sens, bb, coords, fidx, targ, w1, b1, b2, d_scr,
     wbuf, w2buf, row8, prodsend, prodbuf, pf, latbuf, lf, sensend, sgbuf, sgf,
     hid, omh, msgf, msg, rsbuf, agbuf, hf,
-    wsem, w2sem, psend, precv, lsend, lrecv, ssend, srecv, rsend, rrecv, asend, arecv,
+    insem, wsem, w2sem, psend, precv, lsend, lrecv, ssend, srecv, rsend, rrecv, asend, arecv,
     dsend, drecv,
 ):
     branch = lax.axis_index("branch")
@@ -48,9 +47,12 @@
     scale = 1.0 / 32.0
     rows = bw.shape[1] // CHUNKS
 
+    def far(t):
+        return t + lax.div(t, 2) - 2 * lax.div(t, 3)
+
     def peer(d):
         dl, dq = lax.div(d, 32), lax.rem(d, 32)
-        dh, dx, dy = lax.div(dq, 16), lax.rem(lax.div(dq, 4), 4), lax.rem(dq, 4)
+        dh, dx, dy = lax.div(dq, 16), far(lax.rem(lax.div(dq, 4), 4)), far(lax.rem(dq, 4))
         pz = lax.rem(zlo + dl, 2)
         pq = lax.rem(zhi + dh, 2) * 16 + lax.rem(x + dx, 4) * 4 + lax.rem(y + dy, 4)
         return pz * 2 + core, pq
@@ -62,9 +64,17 @@
         part = pl.ds(c * rows, rows)
         return pltpu.make_async_copy(bw.at[k, part], wbuf.at[k, part], wsem.at[k, c])
 
+    smalls = ((sens_hbm, sens), (bb_hbm, bb), (coords_hbm, coords), (w1_hbm, w1), (b1_hbm, b1),
+              (fidx_hbm, fidx), (targ_hbm, targ), (b2_hbm, b2))
+    loads = [pltpu.make_async_copy(a, b, insem.at[i]) for i, (a, b) in enumerate(smalls)]
+    loads[0].start()
+    wcopy(0, 0).start()
+    for load in loads[1:]:
+        load.start()
     for k in range(3):
         for c in range(CHUNKS):
-            wcopy(k, c).start()
+            if k + c:
+                wcopy(k, c).start()
     w2copy = pltpu.make_async_copy(w2, w2buf, w2sem)
     w2copy.start()
 
@@ -99,21 +109,21 @@
             device_id=partner, device_id_type=pl.DeviceIdType.MESH,
         )
 
-    for k in range(3):
-        sk = sens[k].astype(F32)
+    loads[0].wait()
+    for k in range(3):
+        sk = sens[k : k + 1, :].astype(F32)
         for j in range(16):
             sgf[4 * j + k : 4 * j + k + 1, :] = sk[:, 128 * j : 128 * (j + 1)]
     for j in range(16):
         sensend[j] = sgf[4 * j : 4 * j + 4, :].astype(BF16)
 
-    lats = []
+    loads[1].wait()
     for k in range(3):
         pre = bb[k : k + 1, :]
         for c in range(CHUNKS):
             wcopy(k, c).wait()
-            pre = pre + nn(sens[k][:, c * rows : (c + 1) * rows], wbuf[k, c * rows : (c + 1) * rows, :])
+            pre = pre + nn(sens[k : k + 1, c * rows : (c + 1) * rows], wbuf[k, c * rows : (c + 1) * rows, :])
         lat = jnp.tanh(pre).astype(BF16).astype(F32)
-        lats.append(lat)
         for j in range(8):
             row8[k, j : j + 1, :] = lat[:, 128 * j : 128 * (j + 1)]
         latbuf[mine, k] = row8[k].astype(BF16)
@@ -128,6 +138,8 @@
     to_peers(1, 64, lambda d: sensend.at[lax.div(d[1], 2)], lambda d: sgbuf.at[mine], ssend, srecv)
     sgbuf[mine] = sensend[lax.div(q, 2)]
 
+    for load in loads[2:]:
+        load.wait()
     for r in range(4):
         part = slice(128 * r, 128 * (r + 1))
         h = jnp.tanh(tn(coords[:, part], w1[...]) + b1[...]).astype(BF16)
@@ -216,105 +228,127 @@
         cols = slice(128 * j, 128 * (j + 1))
         m12, m02, m01 = l1 * l2, l0 * l2, l0 * l1
         p_out[:, cols] = (m01 * l2).astype(BF16)
-        d_out[0, :, cols] = m12 * (1.0 - l0 * l0)
-        d_out[1, :, cols] = m02 * (1.0 - l1 * l1)
-        d_out[2, :, cols] = m01 * (1.0 - l2 * l2)
+        d_scr[0, :, cols] = m12 * (1.0 - l0 * l0)
+        d_scr[1, :, cols] = m02 * (1.0 - l1 * l1)
+        d_scr[2, :, cols] = m01 * (1.0 - l2 * l2)
 
     wait(agbuf.at[pl.ds(0, 63)], arecv)
     swap_h = swap(agbuf, 2)
     swap_h.start()
+
+    def finish(half):
+        base = pl.multiple_of(half * 64, 64)
+
+        def spread_h(i, carry):
+            at = pl.multiple_of(i * 16, 16)
+            hf[pl.ds(at, ROWS), :] = agbuf[base + i].astype(F32)
+            return carry
+
+        lax.fori_loop(0, 64, spread_h, 0, unroll=4)
+        hm = jnp.concatenate([hf[pl.ds(j, 64, stride=16), :].astype(BF16) for j in range(8)], axis=1)
+        sums = hf[pl.ds(9, 64, stride=16), :] + hf[pl.ds(10, 64, stride=16), :]
+        g = hf[pl.ds(8, 64, stride=16), :]
+        here = pl.ds(base, 64)
+        hm_out[here, :] = hm
+        s_out[here, :] = sums
+        gp = nn(hm, w2buf[...]) + sums[:, 0:1] * b2[...]
+        for k in range(3):
+            delta_out[k, here, :] = (gp * d_scr[k, here, :]).astype(BF16)
+        return g[0:32] + g[32:64]
+
+    g_own = finish(core)
     wait(prodbuf.at[pl.ds(0, 31)], psend)
     wait(latbuf.at[pl.ds(0, 63)], lsend)
     wait(sgbuf.at[pl.ds(0, 63)], ssend)
     wait(rsbuf.at[pl.ds(0, 31)], rsend)
     wait(agbuf.at[pl.ds(0, 63)], asend)
     swap_h.wait()
-
-    def spread_h(i, carry):
-        at = pl.multiple_of(i * 16, 16)
-        hf[pl.ds(at, ROWS), :] = agbuf[i].astype(F32)
-        return carry
-
-    lax.fori_loop(0, 128, spread_h, 0, unroll=4)
-    for j in range(8):
-        hm_out[:, 128 * j : 128 * (j + 1)] = hf[pl.ds(j, 128, stride=16), :].astype(BF16)
-    s_out[...] = hf[pl.ds(9, 128, stride=16), :] + hf[pl.ds(10, 128, stride=16), :]
-    g = hf[pl.ds(8, 128, stride=16), :]
-    g_out[...] = (g[0:32] + g[32:64]) + (g[64:96] + g[96:128])
+    g_out[...] = g_own + finish(1 - core)
 
 
 def output_kernel(
-    hm, prod, d, sg, s, g, w2, b2,
-    gbw_out, gbb_out, gw1_out, gb1_out, gw2_out, gb2_out, gw2buf, sem,
+    hm, prod, delta, sg, s, g,
+    gbw_out, gbb_out, gw1_out, gb1_out, gw2_out, gb2_out,
+    gbw, gbb, gw1, gb1, gw2, gb2, sem,
 ):
-    def drain(c):
+    copies = []
+
+    def drain(source, target):
+        copies.append(pltpu.make_async_copy(source, target, sem.at[len(copies)]))
+        copies[-1].start()
+
+    for c in range(4):
         part = pl.ds(256 * c, 256)
-        return pltpu.make_async_copy(gw2buf.at[part], gw2_out.at[part], sem.at[c])
-
-    for c in range(4):
-        gw2buf[256 * c : 256 * (c + 1), :] = tn(hm[:, 256 * c : 256 * (c + 1)], prod[...])
-        drain(c).start()
-    sums = s[:, 0:1]
-    gp = nn(hm[...], w2[...]) + sums * b2[...]
-    for k in range(3):
-        delta = (gp * d[k]).astype(BF16)
-        gbw_out[k] = tn(sg[k], delta)[0:64, :]
-        gbb_out[k : k + 1, :] = jnp.sum(delta.astype(F32), axis=0, keepdims=True)
-    gb2_out[...] = jnp.sum(sums * prod[...].astype(F32), axis=0, keepdims=True)
+        gw2[256 * c : 256 * (c + 1), :] = tn(hm[:, 256 * c : 256 * (c + 1)], prod[...])
+        drain(gw2.at[part], gw2_out.at[part])
+    for k in range(3):
+        gbw[k] = tn(sg[k], delta[k])[0:64, :]
+        drain(gbw.at[k], gbw_out.at[k])
+    for k in range(3):
+        gbb[k : k + 1, :] = jnp.sum(delta[k].astype(F32), axis=0, keepdims=True)
+    gb2[...] = jnp.sum(s[:, 0:1] * prod[...].astype(F32), axis=0, keepdims=True)
     for j in range(8):
         cols = slice(128 * j, 128 * (j + 1))
         for c in range(3):
-            gw1_out[c : c + 1, cols] = g[8 * c + j : 8 * c + j + 1, :]
-        gb1_out[:, cols] = g[24 + j : 25 + j, :]
-    for c in range(4):
-        drain(c).wait()
+            gw1[c : c + 1, cols] = g[8 * c + j : 8 * c + j + 1, :]
+        gb1[:, cols] = g[24 + j : 25 + j, :]
+    drain(gbb, gbb_out)
+    drain(gb2, gb2_out)
+    drain(gw1, gw1_out)
+    drain(gb1, gb1_out)
+    for copy in copies:
+        copy.wait()
 
 
 def shards(sensors, branch_w, branch_b, coords, func_index, targets, trunk_w1, trunk_b1, trunk_w2, trunk_b2):
     vmem = pl.BlockSpec(memory_space=pltpu.VMEM)
-    hbm = pl.BlockSpec(memory_space=pl.ANY)
-    b2 = trunk_b2.reshape(1, 1024)
+    hbm = pl.BlockSpec(memory_space=pltpu.HBM)
     shape = jax.ShapeDtypeStruct
     dma = pltpu.SemaphoreType.DMA
-    hm, prod, d, sg, s, g = pl.pallas_call(
+    inputs = (
+        sensors.reshape(3, 2048), branch_w, branch_b, coords, func_index.reshape(1, 512),
+        targets.reshape(1, 512), trunk_w1, trunk_b1.reshape(1, 1024), trunk_w2, trunk_b2.reshape(1, 1024),
+    )
+    passed = pl.pallas_call(
         exchange_kernel,
         out_shape=(
-            shape((128, 1024), BF16), shape((128, 1024), BF16), shape((3, 128, 1024), F32),
+            shape((128, 1024), BF16), shape((128, 1024), BF16), shape((3, 128, 1024), BF16),
             shape((3, 128, 128), BF16), shape((128, 128), F32), shape((32, 128), F32),
         ),
-        in_specs=[vmem, hbm, vmem, vmem, vmem, vmem, vmem, vmem, hbm, vmem],
+        in_specs=[hbm] * 10,
         out_specs=(vmem,) * 6,
         scratch_shapes=[
+            VMEM((3, 2048), BF16), VMEM((3, 1024), F32), VMEM((3, 512), BF16), VMEM((1, 512), jnp.int32),
+            VMEM((1, 512), F32), VMEM((3, 1024), BF16), VMEM((1, 1024), F32), VMEM((1, 1024), F32),
+            VMEM((3, 128, 1024), F32),
             VMEM((3, 2048, 1024), BF16), VMEM((1024, 1024), BF16), VMEM((3, 8, 128), F32),
             VMEM((8, 128), BF16), VMEM((32, 8, 128), BF16), VMEM((256, 128), F32),
             VMEM((128, 3, 8, 128), BF16), VMEM((3, 1024, 128), F32),
             VMEM((16, 4, 128), BF16), VMEM((128, 4, 128), BF16), VMEM((512, 128), F32),
             VMEM((512, 1024), BF16), VMEM((512, 1024), BF16),
             VMEM((512, 128), F32), VMEM((32, ROWS, 128), BF16), VMEM((32, ROWS, 128), BF16),
-            VMEM((128, ROWS, 128), BF16), VMEM((2048, 128), F32),
-            dma((3, CHUNKS)), dma, dma, dma, dma, dma, dma, dma, dma, dma, dma, dma,
+            VMEM((128, ROWS, 128), BF16), VMEM((1024, 128), F32),
+            dma((8,)), dma((3, CHUNKS)), dma, dma, dma, dma, dma, dma, dma, dma, dma, dma, dma,
             dma((3,)), dma((3,)),
         ],
         compiler_params=pltpu.CompilerParams(
             collective_id=0, has_side_effects=True, vmem_limit_bytes=40 * 1024 * 1024
         ),
         name="exchange",
-    )(
-        sensors, branch_w, branch_b, coords, func_index.reshape(1, 512), targets.reshape(1, 512),
-        trunk_w1, trunk_b1.reshape(1, 1024), trunk_w2, b2,
+    )(*[pltpu.with_memory_space_constraint(v, pltpu.HBM) for v in inputs])
+    results = (
+        shape((3, 64, 1024), F32), shape((3, 1024), F32), shape((3, 1024), F32),
+        shape((1, 1024), F32), shape((1024, 1024), F32), shape((1, 1024), F32),
     )
     gbw, gbb, gw1, gb1, gw2, gb2 = pl.pallas_call(
         output_kernel,
-        out_shape=(
-            shape((3, 64, 1024), F32), shape((3, 1024), F32), shape((3, 1024), F32),
-            shape((1, 1024), F32), shape((1024, 1024), F32), shape((1, 1024), F32),
-        ),
-        in_specs=[vmem] * 8,
-        out_specs=(vmem, vmem, vmem, vmem, hbm, vmem),
-        scratch_shapes=[VMEM((1024, 1024), F32), dma((4,))],
-        compiler_params=pltpu.CompilerParams(vmem_limit_bytes=32 * 1024 * 1024),
+        out_shape=results,
+        in_specs=[vmem] * 6,
+        out_specs=(hbm,) * 6,
+        scratch_shapes=[VMEM(r.shape, F32) for r in results] + [dma((11,))],
+        compiler_params=pltpu.CompilerParams(vmem_limit_bytes=16 * 1024 * 1024),
         name="outputs",
-    )(hm, prod, d, sg, s, g, trunk_w2, b2)
+    )(*passed)
     return gbw, gbb, gw1, gb1.reshape(1024), gw2, gb2.reshape(1024)
 
 

time: 45.5 us -> 38.2 us (0.84)
  local copies, waits for them, and re-layouts: 7.16 us -> 0 us
    unnamed x17 -> x0, local copies, waits for them, and re-layouts: 7.16 us -> none
    pallas_call x1, Pallas kernels: 33.9 us -> 34.8 us  [shards(): pl.pallas_call(exchange_kernel, out_shape=(shape((128, 1024), BF16), shap...]
    pallas_call x1, Pallas kernels: 3.26 us -> 2.67 us  [shards(): pl.pallas_call(output_kernel, out_shape=results, in_specs=[vmem] * 6, out...]
where the time goes in v2:
time: 38.2 us; the launch traced here: 38.1 us
  Pallas kernels  37.4 us (98%)
  between operations  0.64 us (2%)
    pallas_call x1, Pallas kernels, shards(): pl.pallas_call(exchange_kernel, out_shape=(shape((128, 1024), BF16), shap...  34.8 us
    pallas_call x1, Pallas kernels, shards(): pl.pallas_call(output_kernel, out_shape=results, in_specs=[vmem] * 6, out...  2.67 us

profile of v2, /device:TPU:1, one launch (start us, length us, event | category | flops | bytes accessed | tf_op | source)
XLA Modules:
  0.0 38.1 jit_solution(12252131401630527470)
XLA Ops:
  0.6 34.8 %exchange.1 = (bf16[128,1024]{1,0:T(8,128)(2,1)S(1)}, bf16[128,1024]{1,0:T(8,128)(2,1)S(1)}, bf16[3,128,1024]{2,1,0:T(8,128)(2,1)S(1)}, bf16[3,128,128]{2,1,0:T(...) custom-call(bf16[3,2048]{1,0:T(4,128)(2,1)} %bitcast.7, bf16[3,2048,1024]{2,1,0:T(8,128)(2,1)} %bw.1, ...), custom_call_target="tpu_custom_call" | custom-call | tf_op jit(solution)/shard_map/exchange/pallas_call | solution.py:312
  35.4 2.7 %outputs.1 = (f32[3,64,1024]{2,1,0:T(8,128)}, f32[3,1024]{1,0:T(4,128)}, f32[3,1024]{1,0:T(4,128)}, f32[1,1024]{1,0:T(1,128)}, f32[1024,1024]{1,0:T(8,128)}, /*index=5*/f32[1,1024]{1,0:T(1,128)}) custom-call(bf16[128,1024]{1,0:T(8,128)(2,1)S(1)} %get-tuple-element.18.hm, bf16[128,1024]{1,0:T(8,128)(2,1)S(1)} %get-tuple-element.19.prod, ...), custom_call_target="tpu_custom_call" | custom-call | tf_op jit(solution)/shard_map/outputs/pallas_call | solution.py:343

commit v3 on v2

--- a/solution.py
+++ b/solution.py
@@ -46,26 +46,27 @@
     x, y = lax.div(xy, 4), lax.rem(xy, 4)
     scale = 1.0 / 32.0
     rows = bw.shape[1] // CHUNKS
-
-    def far(t):
-        return t + lax.div(t, 2) - 2 * lax.div(t, 3)
-
-    def peer(d):
-        dl, dq = lax.div(d, 32), lax.rem(d, 32)
-        dh, dx, dy = lax.div(dq, 16), far(lax.rem(lax.div(dq, 4), 4)), far(lax.rem(dq, 4))
-        pz = lax.rem(zlo + dl, 2)
-        pq = lax.rem(zhi + dh, 2) * 16 + lax.rem(x + dx, 4) * 4 + lax.rem(y + dy, 4)
-        return pz * 2 + core, pq
-
+    base = core * 64 + zlo * 32
+    mine = base + q
+
+    xs = [lax.rem(x + o, 4) * 4 for o in range(4)]
+    ys = [lax.rem(y + o, 4) for o in range(4)]
+    away = sorted(((i, j) for i in range(4) for j in range(4)), key=lambda t: -(t[0] != 0) - (t[0] == 2) - (t[1] != 0) - (t[1] == 2))
+    plane = [xs[i] + ys[j] for i, j in away]
+    here, there = zhi * 16, (1 - zhi) * 16
+    near = [(branch, here + p) for p in plane[:-1]]
+    cross = [(branch, there + p) for p in plane]
+    beside = [((1 - zlo) * 2 + core, here + p) for p in plane]
+    group = [d for pair in zip(cross, near + [None]) for d in pair if d is not None]
+    wide = [d for pair in zip(beside, near + [None]) for d in pair if d is not None]
     partner = (zlo * 2 + (1 - core), q)
-    mine = core * 64 + zlo * 32 + q
 
     def wcopy(k, c):
         part = pl.ds(c * rows, rows)
         return pltpu.make_async_copy(bw.at[k, part], wbuf.at[k, part], wsem.at[k, c])
 
-    smalls = ((sens_hbm, sens), (bb_hbm, bb), (coords_hbm, coords), (w1_hbm, w1), (b1_hbm, b1),
-              (fidx_hbm, fidx), (targ_hbm, targ), (b2_hbm, b2))
+    smalls = ((sens_hbm, sens), (bb_hbm, bb), (coords_hbm, coords.at[0]), (fidx_hbm, fidx.at[0]),
+              (targ_hbm, targ.at[0]), (w1_hbm, w1), (b1_hbm, b1), (b2_hbm, b2))
     loads = [pltpu.make_async_copy(a, b, insem.at[i]) for i, (a, b) in enumerate(smalls)]
     loads[0].start()
     wcopy(0, 0).start()
@@ -79,44 +80,38 @@
     w2copy.start()
 
     barrier = pltpu.get_barrier_semaphore()
-
-    def greet(i, carry):
-        pl.semaphore_signal(barrier, inc=1, device_id=peer(i), device_id_type=pl.DeviceIdType.MESH)
-        return carry
-
-    lax.fori_loop(1, 64, greet, 0)
-    pl.semaphore_signal(barrier, inc=1, device_id=partner, device_id_type=pl.DeviceIdType.MESH)
-
-    def to_peers(lo, hi, source, target, send, recv):
-        def one(i, carry):
-            d = hi - 1 - i
-            device = peer(d)
-            pltpu.make_async_remote_copy(
-                src_ref=source(device), dst_ref=target(device), send_sem=send, recv_sem=recv,
-                device_id=device, device_id_type=pl.DeviceIdType.MESH,
-            ).start()
-            return carry
-
-        lax.fori_loop(0, hi - lo, one, 0)
+    greeted = group + beside + [partner]
+    for device in greeted:
+        pl.semaphore_signal(barrier, inc=1, device_id=device, device_id_type=pl.DeviceIdType.MESH)
+
+    def send(source, target, send_sem, recv_sem, device):
+        pltpu.make_async_remote_copy(
+            src_ref=source, dst_ref=target, send_sem=send_sem, recv_sem=recv_sem,
+            device_id=device, device_id_type=pl.DeviceIdType.MESH,
+        ).start()
 
     def wait(ref, sem):
         pltpu.make_async_copy(ref, ref, sem).wait()
 
+    def handed(ref, i, device):
+        return pltpu.make_async_remote_copy(
+            src_ref=ref[0], dst_ref=ref[1], send_sem=dsend.at[i], recv_sem=drecv.at[i],
+            device_id=device, device_id_type=pl.DeviceIdType.MESH,
+        )
+
     def swap(buf, i):
         half = buf.at[pl.ds(core * 64, 64)]
-        return pltpu.make_async_remote_copy(
-            src_ref=half, dst_ref=half, send_sem=dsend.at[i], recv_sem=drecv.at[i],
-            device_id=partner, device_id_type=pl.DeviceIdType.MESH,
-        )
+        return handed((half, half), i, partner)
+
+    def aside(buf, i):
+        part = buf.at[pl.ds(base, 32)]
+        return handed((part, part), i, ((1 - zlo) * 2 + core, q))
+
+    across = [
+        handed((r.at[0], r.at[1]), i, (branch, there + xy)) for i, r in enumerate((coords, fidx, targ))
+    ]
 
     loads[0].wait()
-    for k in range(3):
-        sk = sens[k : k + 1, :].astype(F32)
-        for j in range(16):
-            sgf[4 * j + k : 4 * j + k + 1, :] = sk[:, 128 * j : 128 * (j + 1)]
-    for j in range(16):
-        sensend[j] = sgf[4 * j : 4 * j + 4, :].astype(BF16)
-
     loads[1].wait()
     for k in range(3):
         pre = bb[k : k + 1, :]
@@ -130,24 +125,47 @@
     own = (row8[0] * row8[1] * row8[2]).astype(BF16)
     prodsend[...] = own
     prodbuf[q] = own
-
-    pl.semaphore_wait(barrier, 64)
-
-    to_peers(1, 32, lambda d: prodsend, lambda d: prodbuf.at[q], psend, precv)
-    to_peers(1, 64, lambda d: latbuf.at[mine], lambda d: latbuf.at[mine], lsend, lrecv)
-    to_peers(1, 64, lambda d: sensend.at[lax.div(d[1], 2)], lambda d: sgbuf.at[mine], ssend, srecv)
-    sgbuf[mine] = sensend[lax.div(q, 2)]
-
     for load in loads[2:]:
         load.wait()
-    for r in range(4):
-        part = slice(128 * r, 128 * (r + 1))
-        h = jnp.tanh(tn(coords[:, part], w1[...]) + b1[...]).astype(BF16)
-        hid[part, :] = h
-        hw = h.astype(F32)
-        omh[part, :] = (1.0 - hw * hw).astype(BF16)
-
-    owned = lax.broadcasted_iota(jnp.int32, (32, 512), 0) == fidx[...]
+
+    pl.semaphore_wait(barrier, len(greeted))
+
+    for device in group:
+        send(prodsend, prodbuf.at[q], psend, precv, device)
+    for copy in across:
+        copy.start()
+    for device in group:
+        send(latbuf.at[mine], latbuf.at[mine], lsend, lrecv, device)
+
+    for k in range(3):
+        sk = sens[k : k + 1, :].astype(F32)
+        for j in range(16):
+            sgf[4 * j + k : 4 * j + k + 1, :] = sk[:, 128 * j : 128 * (j + 1)]
+    for j in range(16):
+        sensend[j] = sgf[4 * j : 4 * j + 4, :].astype(BF16)
+    sgbuf[mine] = sensend[lax.div(q, 2)]
+
+    def layer(which):
+        for r in range(4):
+            h = jnp.tanh(tn(coords[which, :, 128 * r : 128 * (r + 1)], w1[...]) + b1[...]).astype(BF16)
+            at = 512 * which + 128 * r
+            hid[at : at + 128, :] = h
+            hw = h.astype(F32)
+            omh[at : at + 128, :] = (1.0 - hw * hw).astype(BF16)
+
+    layer(0)
+    for device in group:
+        send(sensend.at[lax.div(device[1], 2)], sgbuf.at[mine], ssend, srecv, device)
+    for copy in across:
+        copy.wait()
+    layer(1)
+
+    def points(ref):
+        return jnp.concatenate([ref[0], ref[1]], axis=1)
+
+    owned = lax.broadcasted_iota(jnp.int32, (32, 1024), 0) == points(fidx)
+    target = points(targ)
+    cf = points(coords).astype(F32)
 
     w2copy.wait()
     wait(prodbuf.at[pl.ds(0, 31)], precv)
@@ -160,13 +178,12 @@
     dots = nt(jnp.concatenate([qh, ql], axis=0), hid[...])
     dots = dots[:32] + dots[32:] + shift
     pred = jnp.sum(jnp.where(owned, dots, 0.0), axis=0, keepdims=True) * scale
-    resid = (pred - targ[...]) * (1.0 / 128.0)
+    resid = (pred - target) * (1.0 / 128.0)
     a = jnp.where(owned, resid * scale, 0.0)
     ah, al = split(a)
     hsum = nn(jnp.concatenate([ah, al], axis=0), hid[...])
     hsum = hsum[:32] + hsum[32:]
     asum = jnp.sum(a, axis=1, keepdims=True)
-    cf = coords[...].astype(F32)
     za = jnp.concatenate([a * cf[c : c + 1, :] for c in range(3)] + [a], axis=0).astype(BF16)
     z = nn(za, omh[...])
     gw1 = [jnp.sum(quad * z[32 * c : 32 * c + 32, :], axis=0, keepdims=True) for c in range(4)]
@@ -182,27 +199,38 @@
     for f in range(32):
         msg[f] = msgf[16 * f : 16 * f + ROWS, :].astype(BF16)
 
-    to_peers(1, 32, lambda d: msg.at[d[1]], lambda d: rsbuf.at[q], rsend, rrecv)
-    rsbuf[q] = msg[q]
-
-    wait(latbuf.at[pl.ds(0, 63)], lrecv)
-    wait(sgbuf.at[pl.ds(0, 63)], srecv)
-    swap_lat, swap_sens = swap(latbuf, 0), swap(sgbuf, 1)
+    for device in near:
+        send(msg.at[pl.ds(lax.rem(device[1], 16) * 2, 2)], rsbuf.at[xy], rsend, rrecv, device)
+    rsbuf[xy] = msg[pl.ds(xy * 2, 2)]
+
+    wait(latbuf.at[pl.ds(0, 31)], lrecv)
+    wait(sgbuf.at[pl.ds(0, 31)], srecv)
+    side_lat, side_sens = aside(latbuf, 3), aside(sgbuf, 4)
+    side_lat.start()
+    side_sens.start()
+
+    wait(rsbuf.at[pl.ds(0, 15)], rrecv)
+    total = rsbuf[0].astype(F32)
+    for f in range(1, 16):
+        total = total + rsbuf[f].astype(F32)
+    first = base + xy * 2
+    for r in range(2):
+        at = 16 * r
+        hf[at : at + ROWS, :] = total[r]
+        s = hf[at + 9 : at + 10, :] + hf[at + 10 : at + 11, :]
+        sh = s.astype(BF16).astype(F32)
+        hf[at + 9 : at + 10, :] = sh
+        hf[at + 10 : at + 11, :] = s - sh
+        agbuf[first + r] = hf[at : at + ROWS, :].astype(BF16)
+    pair = agbuf.at[pl.ds(first, 2)]
+    for device in wide:
+        send(pair, pair, asend, arecv, device)
+
+    side_lat.wait()
+    side_sens.wait()
+    swap_lat, swap_sens = swap(latbuf, 5), swap(sgbuf, 6)
     swap_lat.start()
     swap_sens.start()
-
-    wait(rsbuf.at[pl.ds(0, 31)], rrecv)
-    total = rsbuf[0].astype(F32)
-    for f in range(1, 32):
-        total = total + rsbuf[f].astype(F32)
-    hf[0:ROWS, :] = total
-    s = hf[9:10, :] + hf[10:11, :]
-    sh = s.astype(BF16).astype(F32)
-    hf[9:10, :] = sh
-    hf[10:11, :] = s - sh
-    agbuf[mine] = hf[0:ROWS, :].astype(BF16)
-    to_peers(1, 64, lambda d: agbuf.at[mine], lambda d: agbuf.at[mine], asend, arecv)
-
     swap_lat.wait()
     swap_sens.wait()
 
@@ -232,36 +260,36 @@
         d_scr[1, :, cols] = m02 * (1.0 - l1 * l1)
         d_scr[2, :, cols] = m01 * (1.0 - l2 * l2)
 
-    wait(agbuf.at[pl.ds(0, 63)], arecv)
-    swap_h = swap(agbuf, 2)
+    wait(agbuf.at[pl.ds(0, 62)], arecv)
+    swap_h = swap(agbuf, 7)
     swap_h.start()
 
     def finish(half):
-        base = pl.multiple_of(half * 64, 64)
+        start = pl.multiple_of(half * 64, 64)
 
         def spread_h(i, carry):
             at = pl.multiple_of(i * 16, 16)
-            hf[pl.ds(at, ROWS), :] = agbuf[base + i].astype(F32)
+            hf[pl.ds(at, ROWS), :] = agbuf[start + i].astype(F32)
             return carry
 
         lax.fori_loop(0, 64, spread_h, 0, unroll=4)
         hm = jnp.concatenate([hf[pl.ds(j, 64, stride=16), :].astype(BF16) for j in range(8)], axis=1)
         sums = hf[pl.ds(9, 64, stride=16), :] + hf[pl.ds(10, 64, stride=16), :]
         g = hf[pl.ds(8, 64, stride=16), :]
-        here = pl.ds(base, 64)
-        hm_out[here, :] = hm
-        s_out[here, :] = sums
+        part = pl.ds(start, 64)
+        hm_out[part, :] = hm
+        s_out[part, :] = sums
         gp = nn(hm, w2buf[...]) + sums[:, 0:1] * b2[...]
         for k in range(3):
-            delta_out[k, here, :] = (gp * d_scr[k, here, :]).astype(BF16)
+            delta_out[k, part, :] = (gp * d_scr[k, part, :]).astype(BF16)
         return g[0:32] + g[32:64]
 
     g_own = finish(core)
     wait(prodbuf.at[pl.ds(0, 31)], psend)
-    wait(latbuf.at[pl.ds(0, 63)], lsend)
-    wait(sgbuf.at[pl.ds(0, 63)], ssend)
-    wait(rsbuf.at[pl.ds(0, 31)], rsend)
-    wait(agbuf.at[pl.ds(0, 63)], asend)
+    wait(latbuf.at[pl.ds(0, 31)], lsend)
+    wait(sgbuf.at[pl.ds(0, 31)], ssend)
+    wait(rsbuf.at[pl.ds(0, 15)], rsend)
+    wait(agbuf.at[pl.ds(0, 62)], asend)
     swap_h.wait()
     g_out[...] = g_own + finish(1 - core)
 
@@ -318,18 +346,18 @@
         in_specs=[hbm] * 10,
         out_specs=(vmem,) * 6,
         scratch_shapes=[
-            VMEM((3, 2048), BF16), VMEM((3, 1024), F32), VMEM((3, 512), BF16), VMEM((1, 512), jnp.int32),
-            VMEM((1, 512), F32), VMEM((3, 1024), BF16), VMEM((1, 1024), F32), VMEM((1, 1024), F32),
+            VMEM((3, 2048), BF16), VMEM((3, 1024), F32), VMEM((2, 3, 512), BF16), VMEM((2, 1, 512), jnp.int32),
+            VMEM((2, 1, 512), F32), VMEM((3, 1024), BF16), VMEM((1, 1024), F32), VMEM((1, 1024), F32),
             VMEM((3, 128, 1024), F32),
             VMEM((3, 2048, 1024), BF16), VMEM((1024, 1024), BF16), VMEM((3, 8, 128), F32),
             VMEM((8, 128), BF16), VMEM((32, 8, 128), BF16), VMEM((256, 128), F32),
             VMEM((128, 3, 8, 128), BF16), VMEM((3, 1024, 128), F32),
             VMEM((16, 4, 128), BF16), VMEM((128, 4, 128), BF16), VMEM((512, 128), F32),
-            VMEM((512, 1024), BF16), VMEM((512, 1024), BF16),
-            VMEM((512, 128), F32), VMEM((32, ROWS, 128), BF16), VMEM((32, ROWS, 128), BF16),
+            VMEM((1024, 1024), BF16), VMEM((1024, 1024), BF16),
+            VMEM((512, 128), F32), VMEM((32, ROWS, 128), BF16), VMEM((16, 2, ROWS, 128), BF16),
             VMEM((128, ROWS, 128), BF16), VMEM((1024, 128), F32),
             dma((8,)), dma((3, CHUNKS)), dma, dma, dma, dma, dma, dma, dma, dma, dma, dma, dma,
-            dma((3,)), dma((3,)),
+            dma((8,)), dma((8,)),
         ],
         compiler_params=pltpu.CompilerParams(
             collective_id=0, has_side_effects=True, vmem_limit_bytes=40 * 1024 * 1024

time: 38.2 us -> 35.6 us (0.932)
  Pallas kernels: 37.4 us -> 34.8 us
    pallas_call x1, Pallas kernels: 34.8 us -> 32.1 us  [shards(): pl.pallas_call(exchange_kernel, out_shape=(shape((128, 1024), BF16), shap...]
where the time goes in v3:
time: 35.6 us; the launch traced here: 35.5 us
  Pallas kernels  34.8 us (98%)
  between operations  0.64 us (2%)
    pallas_call x1, Pallas kernels, shards(): pl.pallas_call(exchange_kernel, out_shape=(shape((128, 1024), BF16), shap...  32.1 us
    pallas_call x1, Pallas kernels, shards(): pl.pallas_call(output_kernel, out_shape=results, in_specs=[vmem] * 6, out...  2.67 us

profile of v3, /device:TPU:1, one launch (start us, length us, event | category | flops | bytes accessed | tf_op | source)
XLA Modules:
  0.0 35.5 jit_solution(15108954590898329811)
XLA Ops:
  0.6 32.1 %exchange.1 = (bf16[128,1024]{1,0:T(8,128)(2,1)S(1)}, bf16[128,1024]{1,0:T(8,128)(2,1)S(1)}, bf16[3,128,1024]{2,1,0:T(8,128)(2,1)S(1)}, bf16[3,128,128]{2,1,0:T(...) custom-call(bf16[3,2048]{1,0:T(4,128)(2,1)} %bitcast.7, bf16[3,2048,1024]{2,1,0:T(8,128)(2,1)} %bw.1, ...), custom_call_target="tpu_custom_call" | custom-call | tf_op jit(solution)/shard_map/exchange/pallas_call | solution.py:340
  32.8 2.7 %outputs.1 = (f32[3,64,1024]{2,1,0:T(8,128)}, f32[3,1024]{1,0:T(4,128)}, f32[3,1024]{1,0:T(4,128)}, f32[1,1024]{1,0:T(1,128)}, f32[1024,1024]{1,0:T(8,128)}, /*index=5*/f32[1,1024]{1,0:T(1,128)}) custom-call(bf16[128,1024]{1,0:T(8,128)(2,1)S(1)} %get-tuple-element.18.hm, bf16[128,1024]{1,0:T(8,128)(2,1)S(1)} %get-tuple-element.19.prod, ...), custom_call_target="tpu_custom_call" | custom-call | tf_op jit(solution)/shard_map/outputs/pallas_call | solution.py:371

commit v4 on v3

--- a/solution.py
+++ b/solution.py
@@ -7,7 +7,7 @@
 
 F32 = jnp.float32
 BF16 = jnp.bfloat16
-ROWS = 12
+ROWS = 10
 CHUNKS = 4
 VMEM = pltpu.VMEM
 
@@ -31,12 +31,12 @@
 
 def exchange_kernel(
     sens_hbm, bw, bb_hbm, coords_hbm, fidx_hbm, targ_hbm, w1_hbm, b1_hbm, w2, b2_hbm,
-    hm_out, p_out, delta_out, sg_out, s_out, g_out,
-    sens, bb, coords, fidx, targ, w1, b1, b2, d_scr,
-    wbuf, w2buf, row8, prodsend, prodbuf, pf, latbuf, lf, sensend, sgbuf, sgf,
-    hid, omh, msgf, msg, rsbuf, agbuf, hf,
+    hm_out, p_out, d_out, sg_out, s_out, g_out, w2buf, b2,
+    sens, bb, coords, fidx, targ, w1, b1,
+    wbuf, row8, prodsend, prodbuf, pf, latbuf, lf, sensend, sgbuf, sgf,
+    hid, omh, msgf, msg, rsbuf, agbuf, hf, tmsg, trs, tag,
     insem, wsem, w2sem, psend, precv, lsend, lrecv, ssend, srecv, rsend, rrecv, asend, arecv,
-    dsend, drecv,
+    tsend, trecv, usend, urecv, dsend, drecv,
 ):
     branch = lax.axis_index("branch")
     q = lax.axis_index("query")
@@ -56,7 +56,8 @@
     here, there = zhi * 16, (1 - zhi) * 16
     near = [(branch, here + p) for p in plane[:-1]]
     cross = [(branch, there + p) for p in plane]
-    beside = [((1 - zlo) * 2 + core, here + p) for p in plane]
+    other = (1 - zlo) * 2 + core
+    beside = [(other, here + p) for p in plane]
     group = [d for pair in zip(cross, near + [None]) for d in pair if d is not None]
     wide = [d for pair in zip(beside, near + [None]) for d in pair if d is not None]
     partner = (zlo * 2 + (1 - core), q)
@@ -80,7 +81,7 @@
     w2copy.start()
 
     barrier = pltpu.get_barrier_semaphore()
-    greeted = group + beside + [partner]
+    greeted = group + beside + [(other, there + xy), partner]
     for device in greeted:
         pl.semaphore_signal(barrier, inc=1, device_id=device, device_id_type=pl.DeviceIdType.MESH)
 
@@ -99,13 +100,13 @@
             device_id=device, device_id_type=pl.DeviceIdType.MESH,
         )
 
-    def swap(buf, i):
-        half = buf.at[pl.ds(core * 64, 64)]
+    def swap(buf, i, count=64):
+        half = buf.at[pl.ds(core * count, count)]
         return handed((half, half), i, partner)
 
-    def aside(buf, i):
-        part = buf.at[pl.ds(base, 32)]
-        return handed((part, part), i, ((1 - zlo) * 2 + core, q))
+    def aside(buf, i, start, count, where):
+        part = buf.at[pl.ds(start, count)]
+        return handed((part, part), i, (other, where + xy))
 
     across = [
         handed((r.at[0], r.at[1]), i, (branch, there + xy)) for i, r in enumerate((coords, fidx, targ))
@@ -177,6 +178,17 @@
     qh, ql = split(quad)
     dots = nt(jnp.concatenate([qh, ql], axis=0), hid[...])
     dots = dots[:32] + dots[32:] + shift
+
+    wait(sgbuf.at[pl.ds(0, 31)], srecv)
+    wait(latbuf.at[pl.ds(0, 31)], lrecv)
+    sides = [
+        aside(sgbuf, 3, base, 32, here),
+        aside(latbuf, 4, base + here, 16, here),
+        aside(latbuf, 5, base + here, 16, there),
+    ]
+    for copy in sides:
+        copy.start()
+
     pred = jnp.sum(jnp.where(owned, dots, 0.0), axis=0, keepdims=True) * scale
     resid = (pred - target) * (1.0 / 128.0)
     a = jnp.where(owned, resid * scale, 0.0)
@@ -184,18 +196,11 @@
     hsum = nn(jnp.concatenate([ah, al], axis=0), hid[...])
     hsum = hsum[:32] + hsum[32:]
     asum = jnp.sum(a, axis=1, keepdims=True)
-    za = jnp.concatenate([a * cf[c : c + 1, :] for c in range(3)] + [a], axis=0).astype(BF16)
-    z = nn(za, omh[...])
-    gw1 = [jnp.sum(quad * z[32 * c : 32 * c + 32, :], axis=0, keepdims=True) for c in range(4)]
     for j in range(8):
         msgf[pl.ds(j, 32, stride=16), :] = hsum[:, 128 * j : 128 * (j + 1)]
-        for c in range(4):
-            at = 16 * (8 * c + j) + 8
-            msgf[at : at + 1, :] = gw1[c][:, 128 * j : 128 * (j + 1)]
     sh, sl = split(asum)
-    msgf[pl.ds(9, 32, stride=16), :] = jnp.broadcast_to(sh.astype(F32), (32, 128))
-    msgf[pl.ds(10, 32, stride=16), :] = jnp.broadcast_to(sl.astype(F32), (32, 128))
-    msgf[pl.ds(11, 32, stride=16), :] = jnp.zeros((32, 128), F32)
+    msgf[pl.ds(8, 32, stride=16), :] = jnp.broadcast_to(sh.astype(F32), (32, 128))
+    msgf[pl.ds(9, 32, stride=16), :] = jnp.broadcast_to(sl.astype(F32), (32, 128))
     for f in range(32):
         msg[f] = msgf[16 * f : 16 * f + ROWS, :].astype(BF16)
 
@@ -203,11 +208,15 @@
         send(msg.at[pl.ds(lax.rem(device[1], 16) * 2, 2)], rsbuf.at[xy], rsend, rrecv, device)
     rsbuf[xy] = msg[pl.ds(xy * 2, 2)]
 
-    wait(latbuf.at[pl.ds(0, 31)], lrecv)
-    wait(sgbuf.at[pl.ds(0, 31)], srecv)
-    side_lat, side_sens = aside(latbuf, 3), aside(sgbuf, 4)
-    side_lat.start()
-    side_sens.start()
+    za = jnp.concatenate([a * cf[c : c + 1, :] for c in range(3)] + [a], axis=0).astype(BF16)
+    z = nn(za, omh[...])
+    for c in range(4):
+        row = jnp.sum(quad * z[32 * c : 32 * c + 32, :], axis=0, keepdims=True)
+        for j in range(8):
+            tmsg[4 * c + j // 2, j % 2 : j % 2 + 1, :] = row[:, 128 * j : 128 * (j + 1)]
+    for device in near:
+        send(tmsg.at[lax.rem(device[1], 16)], trs.at[xy], tsend, trecv, device)
+    trs[xy] = tmsg[xy]
 
     wait(rsbuf.at[pl.ds(0, 15)], rrecv)
     total = rsbuf[0].astype(F32)
@@ -217,20 +226,30 @@
     for r in range(2):
         at = 16 * r
         hf[at : at + ROWS, :] = total[r]
-        s = hf[at + 9 : at + 10, :] + hf[at + 10 : at + 11, :]
+        s = hf[at + 8 : at + 9, :] + hf[at + 9 : at + 10, :]
         sh = s.astype(BF16).astype(F32)
-        hf[at + 9 : at + 10, :] = sh
-        hf[at + 10 : at + 11, :] = s - sh
+        hf[at + 8 : at + 9, :] = sh
+        hf[at + 9 : at + 10, :] = s - sh
         agbuf[first + r] = hf[at : at + ROWS, :].astype(BF16)
     pair = agbuf.at[pl.ds(first, 2)]
     for device in wide:
         send(pair, pair, asend, arecv, device)
 
-    side_lat.wait()
-    side_sens.wait()
-    swap_lat, swap_sens = swap(latbuf, 5), swap(sgbuf, 6)
+    for copy in sides:
+        copy.wait()
+    swap_lat, swap_sens = swap(latbuf, 6), swap(sgbuf, 7)
     swap_lat.start()
     swap_sens.start()
+
+    wait(trs.at[pl.ds(0, 15)], trecv)
+    tsum = trs[0]
+    for f in range(1, 16):
+        tsum = tsum + trs[f]
+    tmine = tag.at[core * 32 + zlo * 16 + xy]
+    tmine[...] = tsum
+    for device in wide:
+        send(tmine, tmine, usend, urecv, device)
+
     swap_lat.wait()
     swap_sens.wait()
 
@@ -256,15 +275,15 @@
         cols = slice(128 * j, 128 * (j + 1))
         m12, m02, m01 = l1 * l2, l0 * l2, l0 * l1
         p_out[:, cols] = (m01 * l2).astype(BF16)
-        d_scr[0, :, cols] = m12 * (1.0 - l0 * l0)
-        d_scr[1, :, cols] = m02 * (1.0 - l1 * l1)
-        d_scr[2, :, cols] = m01 * (1.0 - l2 * l2)
+        d_out[0, :, cols] = m12 * (1.0 - l0 * l0)
+        d_out[1, :, cols] = m02 * (1.0 - l1 * l1)
+        d_out[2, :, cols] = m01 * (1.0 - l2 * l2)
 
     wait(agbuf.at[pl.ds(0, 62)], arecv)
-    swap_h = swap(agbuf, 7)
+    swap_h = swap(agbuf, 8)
     swap_h.start()
 
-    def finish(half):
+    def arrange(half):
         start = pl.multiple_of(half * 64, 64)
 
         def spread_h(i, carry):
@@ -272,30 +291,31 @@
             hf[pl.ds(at, ROWS), :] = agbuf[start + i].astype(F32)
             return carry
 
-        lax.fori_loop(0, 64, spread_h, 0, unroll=4)
-        hm = jnp.concatenate([hf[pl.ds(j, 64, stride=16), :].astype(BF16) for j in range(8)], axis=1)
-        sums = hf[pl.ds(9, 64, stride=16), :] + hf[pl.ds(10, 64, stride=16), :]
-        g = hf[pl.ds(8, 64, stride=16), :]
+        lax.fori_loop(0, 64, spread_h, 0, unroll=8)
         part = pl.ds(start, 64)
-        hm_out[part, :] = hm
-        s_out[part, :] = sums
-        gp = nn(hm, w2buf[...]) + sums[:, 0:1] * b2[...]
-        for k in range(3):
-            delta_out[k, part, :] = (gp * d_scr[k, part, :]).astype(BF16)
-        return g[0:32] + g[32:64]
-
-    g_own = finish(core)
+        for j in range(8):
+            hm_out[part, 128 * j : 128 * (j + 1)] = hf[pl.ds(j, 64, stride=16), :].astype(BF16)
+        s_out[part, :] = hf[pl.ds(8, 64, stride=16), :] + hf[pl.ds(9, 64, stride=16), :]
+
+    arrange(core)
+    wait(tag.at[pl.ds(0, 31)], urecv)
+    swap_t = swap(tag, 9, 32)
+    swap_t.start()
     wait(prodbuf.at[pl.ds(0, 31)], psend)
     wait(latbuf.at[pl.ds(0, 31)], lsend)
     wait(sgbuf.at[pl.ds(0, 31)], ssend)
     wait(rsbuf.at[pl.ds(0, 15)], rsend)
+    wait(trs.at[pl.ds(0, 15)], tsend)
     wait(agbuf.at[pl.ds(0, 62)], asend)
+    wait(tag.at[pl.ds(0, 31)], usend)
     swap_h.wait()
-    g_out[...] = g_own + finish(1 - core)
+    arrange(1 - core)
+    swap_t.wait()
+    g_out[...] = (tag[0:16] + tag[16:32]) + (tag[32:48] + tag[48:64])
 
 
 def output_kernel(
-    hm, prod, delta, sg, s, g,
+    hm, prod, d, sg, s, g, w2, b2,
     gbw_out, gbb_out, gw1_out, gb1_out, gw2_out, gb2_out,
     gbw, gbb, gw1, gb1, gw2, gb2, sem,
 ):
@@ -305,23 +325,30 @@
         copies.append(pltpu.make_async_copy(source, target, sem.at[len(copies)]))
         copies[-1].start()
 
-    for c in range(4):
+    def trunk(c):
         part = pl.ds(256 * c, 256)
         gw2[256 * c : 256 * (c + 1), :] = tn(hm[:, 256 * c : 256 * (c + 1)], prod[...])
         drain(gw2.at[part], gw2_out.at[part])
+
+    trunk(0)
+    trunk(1)
+    sums = s[:, 0:1]
+    gp = nn(hm[...], w2[...]) + sums * b2[...]
+    trunk(2)
+    trunk(3)
     for k in range(3):
-        gbw[k] = tn(sg[k], delta[k])[0:64, :]
+        delta = (gp * d[k]).astype(BF16)
+        gbw[k] = tn(sg[k], delta)[0:64, :]
         drain(gbw.at[k], gbw_out.at[k])
-    for k in range(3):
-        gbb[k : k + 1, :] = jnp.sum(delta[k].astype(F32), axis=0, keepdims=True)
-    gb2[...] = jnp.sum(s[:, 0:1] * prod[...].astype(F32), axis=0, keepdims=True)
+        gbb[k : k + 1, :] = jnp.sum(delta.astype(F32), axis=0, keepdims=True)
+    drain(gbb, gbb_out)
+    gb2[...] = jnp.sum(sums * prod[...].astype(F32), axis=0, keepdims=True)
+    drain(gb2, gb2_out)
     for j in range(8):
         cols = slice(128 * j, 128 * (j + 1))
         for c in range(3):
-            gw1[c : c + 1, cols] = g[8 * c + j : 8 * c + j + 1, :]
-        gb1[:, cols] = g[24 + j : 25 + j, :]
-    drain(gbb, gbb_out)
-    drain(gb2, gb2_out)
+            gw1[c : c + 1, cols] = g[4 * c + j // 2, j % 2 : j % 2 + 1, :]
+        gb1[:, cols] = g[12 + j // 2, j % 2 : j % 2 + 1, :]
     drain(gw1, gw1_out)
     drain(gb1, gb1_out)
     for copy in copies:
@@ -340,24 +367,25 @@
     passed = pl.pallas_call(
         exchange_kernel,
         out_shape=(
-            shape((128, 1024), BF16), shape((128, 1024), BF16), shape((3, 128, 1024), BF16),
-            shape((3, 128, 128), BF16), shape((128, 128), F32), shape((32, 128), F32),
+            shape((128, 1024), BF16), shape((128, 1024), BF16), shape((3, 128, 1024), F32),
+            shape((3, 128, 128), BF16), shape((128, 128), F32), shape((16, 2, 128), F32),
+            shape((1024, 1024), BF16), shape((1, 1024), F32),
         ),
         in_specs=[hbm] * 10,
-        out_specs=(vmem,) * 6,
+        out_specs=(vmem,) * 8,
         scratch_shapes=[
             VMEM((3, 2048), BF16), VMEM((3, 1024), F32), VMEM((2, 3, 512), BF16), VMEM((2, 1, 512), jnp.int32),
-            VMEM((2, 1, 512), F32), VMEM((3, 1024), BF16), VMEM((1, 1024), F32), VMEM((1, 1024), F32),
-            VMEM((3, 128, 1024), F32),
-            VMEM((3, 2048, 1024), BF16), VMEM((1024, 1024), BF16), VMEM((3, 8, 128), F32),
+            VMEM((2, 1, 512), F32), VMEM((3, 1024), BF16), VMEM((1, 1024), F32),
+            VMEM((3, 2048, 1024), BF16), VMEM((3, 8, 128), F32),
             VMEM((8, 128), BF16), VMEM((32, 8, 128), BF16), VMEM((256, 128), F32),
             VMEM((128, 3, 8, 128), BF16), VMEM((3, 1024, 128), F32),
             VMEM((16, 4, 128), BF16), VMEM((128, 4, 128), BF16), VMEM((512, 128), F32),
             VMEM((1024, 1024), BF16), VMEM((1024, 1024), BF16),
             VMEM((512, 128), F32), VMEM((32, ROWS, 128), BF16), VMEM((16, 2, ROWS, 128), BF16),
             VMEM((128, ROWS, 128), BF16), VMEM((1024, 128), F32),
+            VMEM((16, 2, 128), F32), VMEM((16, 2, 128), F32), VMEM((64, 2, 128), F32),
             dma((8,)), dma((3, CHUNKS)), dma, dma, dma, dma, dma, dma, dma, dma, dma, dma, dma,
-            dma((8,)), dma((8,)),
+            dma, dma, dma, dma, dma((10,)), dma((10,)),
         ],
         compiler_params=pltpu.CompilerParams(
             collective_id=0, has_side_effects=True, vmem_limit_bytes=40 * 1024 * 1024
@@ -371,7 +399,7 @@
     gbw, gbb, gw1, gb1, gw2, gb2 = pl.pallas_call(
         output_kernel,
         out_shape=results,
-        in_specs=[vmem] * 6,
+        in_specs=[vmem] * 8,
         out_specs=(hbm,) * 6,
         scratch_shapes=[VMEM(r.shape, F32) for r in results] + [dma((11,))],
         compiler_params=pltpu.CompilerParams(vmem_limit_bytes=16 * 1024 * 1024),

time: 35.6 us -> 35.9 us (level)
  no operation moved by 1% of the time
where the time goes in v4:
time: 35.9 us; the launch traced here: 35.8 us
  Pallas kernels  35.1 us (98%)
  between operations  0.64 us (2%)
    pallas_call x1, Pallas kernels, shards(): pl.pallas_call(exchange_kernel, out_shape=(shape((128, 1024), BF16), shap...  32.5 us
    pallas_call x1, Pallas kernels, shards(): pl.pallas_call(output_kernel, out_shape=results, in_specs=[vmem] * 8, out...  2.67 us

profile of v4, /device:TPU:1, one launch (start us, length us, event | category | flops | bytes accessed | tf_op | source)
XLA Modules:
  0.0 35.8 jit_solution(17145237066216445032)
XLA Ops:
  0.6 32.5 %exchange.1 = (bf16[128,1024]{1,0:T(8,128)(2,1)S(1)}, bf16[128,1024]{1,0:T(8,128)(2,1)S(1)}, f32[3,128,1024]{2,1,0:T(8,128)S(1)}, bf16[3,128,128]{2,1,0:T(8,128)...) custom-call(bf16[3,2048]{1,0:T(4,128)(2,1)} %bitcast.7, ...), custom_call_target="tpu_custom_call" | custom-call | tf_op jit(solution)/shard_map/exchange/pallas_call | solution.py:367
  33.1 2.7 %outputs.1 = (f32[3,64,1024]{2,1,0:T(8,128)}, f32[3,1024]{1,0:T(4,128)}, f32[3,1024]{1,0:T(4,128)}, f32[1,1024]{1,0:T(1,128)}, f32[1024,1024]{1,0:T(8,128)}, /*index=5*/f32[1,1024]{1,0:T(1,128)}) custom-call(bf16[128,1024]{1,0:T(8,128)(2,1)S(1)} %get-tuple-element.20.hm, bf16[128,1024]{1,0:T(8,128)(2,1)S(1)} %get-tuple-element.21.prod, ...), custom_call_target="tpu_custom_call" | custom-call | tf_op jit(solution)/shard_map/outputs/pallas_call | solution.py:399

commit v5 on v4

--- a/solution.py
+++ b/solution.py
@@ -7,8 +7,7 @@
 
 F32 = jnp.float32
 BF16 = jnp.bfloat16
-ROWS = 10
-CHUNKS = 4
+CHUNKS = 2
 VMEM = pltpu.VMEM
 
 
@@ -34,7 +33,7 @@
     hm_out, p_out, d_out, sg_out, s_out, g_out, w2buf, b2,
     sens, bb, coords, fidx, targ, w1, b1,
     wbuf, row8, prodsend, prodbuf, pf, latbuf, lf, sensend, sgbuf, sgf,
-    hid, omh, msgf, msg, rsbuf, agbuf, hf, tmsg, trs, tag,
+    hid, omh, msgf, msg, rsbuf, agbuf, hf, tmsg, trs, tag, tf, srow,
     insem, wsem, w2sem, psend, precv, lsend, lrecv, ssend, srecv, rsend, rrecv, asend, arecv,
     tsend, trecv, usend, urecv, dsend, drecv,
 ):
@@ -81,7 +80,8 @@
     w2copy.start()
 
     barrier = pltpu.get_barrier_semaphore()
-    greeted = group + beside + [(other, there + xy), partner]
+    facing = [(b + 1 - 2 * core, p) for b, p in wide] + [partner]
+    greeted = group + beside + [(other, there + xy)] + facing
     for device in greeted:
         pl.semaphore_signal(barrier, inc=1, device_id=device, device_id_type=pl.DeviceIdType.MESH)
 
@@ -178,6 +178,39 @@
     qh, ql = split(quad)
     dots = nt(jnp.concatenate([qh, ql], axis=0), hid[...])
     dots = dots[:32] + dots[32:] + shift
+    pred = jnp.sum(jnp.where(owned, dots, 0.0), axis=0, keepdims=True) * scale
+    resid = (pred - target) * (1.0 / 128.0)
+    a = jnp.where(owned, resid * scale, 0.0)
+    ah, al = split(a)
+    hsum = nn(jnp.concatenate([ah, al], axis=0), hid[...])
+    hsum = hsum[:32] + hsum[32:]
+    for j in range(8):
+        msgf[pl.ds(j, 32, stride=8), :] = hsum[:, 128 * j : 128 * (j + 1)]
+    for f in range(32):
+        msg[f] = msgf[8 * f : 8 * f + 8, :].astype(BF16)
+
+    for device in near:
+        send(msg.at[pl.ds(lax.rem(device[1], 16) * 2, 2)], rsbuf.at[xy], rsend, rrecv, device)
+    rsbuf[xy] = msg[pl.ds(xy * 2, 2)]
+
+    za = jnp.concatenate([a * cf[c : c + 1, :] for c in range(3)] + [a], axis=0).astype(BF16)
+    z = nn(za, omh[...])
+    for c in range(4):
+        row = jnp.sum(quad * z[32 * c : 32 * c + 32, :], axis=0, keepdims=True)
+        for j in range(8):
+            at = 4 * (4 * c + j // 2) + j % 2
+            tf[at : at + 1, :] = row[:, 128 * j : 128 * (j + 1)]
+    srow[...] = jnp.broadcast_to(jnp.sum(a, axis=1, keepdims=True), (32, 128))
+    left = lax.broadcasted_iota(jnp.int32, (1, 128), 1) < 64
+    for j in range(16):
+        s = jnp.where(left, srow[2 * j : 2 * j + 1, :], srow[2 * j + 1 : 2 * j + 2, :])
+        sh = s.astype(BF16).astype(F32)
+        tf[4 * j + 2 : 4 * j + 3, :] = sh
+        tf[4 * j + 3 : 4 * j + 4, :] = s - sh
+        tmsg[j] = tf[4 * j : 4 * j + 4, :].astype(BF16)
+    for device in near:
+        send(tmsg.at[lax.rem(device[1], 16)], trs.at[xy], tsend, trecv, device)
+    trs[xy] = tmsg[xy]
 
     wait(sgbuf.at[pl.ds(0, 31)], srecv)
     wait(latbuf.at[pl.ds(0, 31)], lrecv)
@@ -189,67 +222,35 @@
     for copy in sides:
         copy.start()
 
-    pred = jnp.sum(jnp.where(owned, dots, 0.0), axis=0, keepdims=True) * scale
-    resid = (pred - target) * (1.0 / 128.0)
-    a = jnp.where(owned, resid * scale, 0.0)
-    ah, al = split(a)
-    hsum = nn(jnp.concatenate([ah, al], axis=0), hid[...])
-    hsum = hsum[:32] + hsum[32:]
-    asum = jnp.sum(a, axis=1, keepdims=True)
-    for j in range(8):
-        msgf[pl.ds(j, 32, stride=16), :] = hsum[:, 128 * j : 128 * (j + 1)]
-    sh, sl = split(asum)
-    msgf[pl.ds(8, 32, stride=16), :] = jnp.broadcast_to(sh.astype(F32), (32, 128))
-    msgf[pl.ds(9, 32, stride=16), :] = jnp.broadcast_to(sl.astype(F32), (32, 128))
-    for f in range(32):
-        msg[f] = msgf[16 * f : 16 * f + ROWS, :].astype(BF16)
-
-    for device in near:
-        send(msg.at[pl.ds(lax.rem(device[1], 16) * 2, 2)], rsbuf.at[xy], rsend, rrecv, device)
-    rsbuf[xy] = msg[pl.ds(xy * 2, 2)]
-
-    za = jnp.concatenate([a * cf[c : c + 1, :] for c in range(3)] + [a], axis=0).astype(BF16)
-    z = nn(za, omh[...])
-    for c in range(4):
-        row = jnp.sum(quad * z[32 * c : 32 * c + 32, :], axis=0, keepdims=True)
-        for j in range(8):
-            tmsg[4 * c + j // 2, j % 2 : j % 2 + 1, :] = row[:, 128 * j : 128 * (j + 1)]
-    for device in near:
-        send(tmsg.at[lax.rem(device[1], 16)], trs.at[xy], tsend, trecv, device)
-    trs[xy] = tmsg[xy]
-
     wait(rsbuf.at[pl.ds(0, 15)], rrecv)
     total = rsbuf[0].astype(F32)
     for f in range(1, 16):
         total = total + rsbuf[f].astype(F32)
     first = base + xy * 2
-    for r in range(2):
-        at = 16 * r
-        hf[at : at + ROWS, :] = total[r]
-        s = hf[at + 8 : at + 9, :] + hf[at + 9 : at + 10, :]
-        sh = s.astype(BF16).astype(F32)
-        hf[at + 8 : at + 9, :] = sh
-        hf[at + 9 : at + 10, :] = s - sh
-        agbuf[first + r] = hf[at : at + ROWS, :].astype(BF16)
+    agbuf[pl.ds(first, 2)] = total.astype(BF16)
     pair = agbuf.at[pl.ds(first, 2)]
     for device in wide:
         send(pair, pair, asend, arecv, device)
+
+    wait(trs.at[pl.ds(0, 15)], trecv)
+    tsum = trs[0].astype(F32)
+    for f in range(1, 16):
+        tsum = tsum + trs[f].astype(F32)
+    tf[0:4, :] = tsum
+    s = tf[2:3, :] + tf[3:4, :]
+    sh = s.astype(BF16).astype(F32)
+    tf[2:3, :] = sh
+    tf[3:4, :] = s - sh
+    tmine = tag.at[core * 32 + zlo * 16 + xy]
+    tmine[...] = tf[0:4, :].astype(BF16)
+    for device in wide + facing:
+        send(tmine, tmine, usend, urecv, device)
 
     for copy in sides:
         copy.wait()
     swap_lat, swap_sens = swap(latbuf, 6), swap(sgbuf, 7)
     swap_lat.start()
     swap_sens.start()
-
-    wait(trs.at[pl.ds(0, 15)], trecv)
-    tsum = trs[0]
-    for f in range(1, 16):
-        tsum = tsum + trs[f]
-    tmine = tag.at[core * 32 + zlo * 16 + xy]
-    tmine[...] = tsum
-    for device in wide:
-        send(tmine, tmine, usend, urecv, device)
-
     swap_lat.wait()
     swap_sens.wait()
 
@@ -287,31 +288,33 @@
         start = pl.multiple_of(half * 64, 64)
 
         def spread_h(i, carry):
-            at = pl.multiple_of(i * 16, 16)
-            hf[pl.ds(at, ROWS), :] = agbuf[start + i].astype(F32)
+            at = pl.multiple_of(i * 8, 8)
+            hf[pl.ds(at, 8), :] = agbuf[start + i].astype(F32)
             return carry
 
         lax.fori_loop(0, 64, spread_h, 0, unroll=8)
-        part = pl.ds(start, 64)
         for j in range(8):
-            hm_out[part, 128 * j : 128 * (j + 1)] = hf[pl.ds(j, 64, stride=16), :].astype(BF16)
-        s_out[part, :] = hf[pl.ds(8, 64, stride=16), :] + hf[pl.ds(9, 64, stride=16), :]
+            hm_out[pl.ds(start, 64), 128 * j : 128 * (j + 1)] = hf[pl.ds(j, 64, stride=8), :].astype(BF16)
 
     arrange(core)
-    wait(tag.at[pl.ds(0, 31)], urecv)
-    swap_t = swap(tag, 9, 32)
-    swap_t.start()
     wait(prodbuf.at[pl.ds(0, 31)], psend)
     wait(latbuf.at[pl.ds(0, 31)], lsend)
     wait(sgbuf.at[pl.ds(0, 31)], ssend)
     wait(rsbuf.at[pl.ds(0, 15)], rsend)
     wait(trs.at[pl.ds(0, 15)], tsend)
     wait(agbuf.at[pl.ds(0, 62)], asend)
-    wait(tag.at[pl.ds(0, 31)], usend)
+    wait(tag.at[pl.ds(0, 63)], usend)
+    wait(tag.at[pl.ds(0, 63)], urecv)
+    for i in range(64):
+        tf[4 * i : 4 * i + 4, :] = tag[i].astype(F32)
+    for r in range(2):
+        g = tf[pl.ds(r, 64, stride=4), :]
+        g_out[r] = (g[0:16] + g[16:32]) + (g[32:48] + g[48:64])
+    s = tf[pl.ds(2, 64, stride=4), :] + tf[pl.ds(3, 64, stride=4), :]
+    s_out[pl.ds(0, 64, stride=2), :] = s
+    s_out[pl.ds(1, 64, stride=2), :] = pltpu.roll(s, 64, 1)
     swap_h.wait()
     arrange(1 - core)
-    swap_t.wait()
-    g_out[...] = (tag[0:16] + tag[16:32]) + (tag[32:48] + tag[48:64])
 
 
 def output_kernel(
@@ -347,8 +350,8 @@
     for j in range(8):
         cols = slice(128 * j, 128 * (j + 1))
         for c in range(3):
-            gw1[c : c + 1, cols] = g[4 * c + j // 2, j % 2 : j % 2 + 1, :]
-        gb1[:, cols] = g[12 + j // 2, j % 2 : j % 2 + 1, :]
+            gw1[c : c + 1, cols] = g[j % 2, 4 * c + j // 2 : 4 * c + j // 2 + 1, :]
+        gb1[:, cols] = g[j % 2, 12 + j // 2 : 13 + j // 2, :]
     drain(gw1, gw1_out)
     drain(gb1, gb1_out)
     for copy in copies:
@@ -368,7 +371,7 @@
         exchange_kernel,
         out_shape=(
             shape((128, 1024), BF16), shape((128, 1024), BF16), shape((3, 128, 1024), F32),
-            shape((3, 128, 128), BF16), shape((128, 128), F32), shape((16, 2, 128), F32),
+            shape((3, 128, 128), BF16), shape((128, 128), F32), shape((2, 16, 128), F32),
             shape((1024, 1024), BF16), shape((1, 1024), F32),
         ),
         in_specs=[hbm] * 10,
@@ -381,9 +384,10 @@
             VMEM((128, 3, 8, 128), BF16), VMEM((3, 1024, 128), F32),
             VMEM((16, 4, 128), BF16), VMEM((128, 4, 128), BF16), VMEM((512, 128), F32),
             VMEM((1024, 1024), BF16), VMEM((1024, 1024), BF16),
-            VMEM((512, 128), F32), VMEM((32, ROWS, 128), BF16), VMEM((16, 2, ROWS, 128), BF16),
-            VMEM((128, ROWS, 128), BF16), VMEM((1024, 128), F32),
-            VMEM((16, 2, 128), F32), VMEM((16, 2, 128), F32), VMEM((64, 2, 128), F32),
+            VMEM((256, 128), F32), VMEM((32, 8, 128), BF16), VMEM((16, 2, 8, 128), BF16),
+            VMEM((128, 8, 128), BF16), VMEM((512, 128), F32),
+            VMEM((16, 4, 128), BF16), VMEM((16, 4, 128), BF16), VMEM((64, 4, 128), BF16),
+            VMEM((256, 128), F32), VMEM((32, 128), F32),
             dma((8,)), dma((3, CHUNKS)), dma, dma, dma, dma, dma, dma, dma, dma, dma, dma, dma,
             dma, dma, dma, dma, dma((10,)), dma((10,)),
         ],

time: 35.9 us -> 33.9 us (0.944)
  Pallas kernels: 35.1 us -> 33.1 us
    pallas_call x1, Pallas kernels: 32.5 us -> 30.5 us  [shards(): pl.pallas_call(exchange_kernel, out_shape=(shape((128, 1024), BF16), shap...]
where the time goes in v5:
time: 33.9 us; the launch traced here: 33.8 us
  Pallas kernels  33.1 us (98%)
  between operations  0.64 us (2%)
    pallas_call x1, Pallas kernels, shards(): pl.pallas_call(exchange_kernel, out_shape=(shape((128, 1024), BF16), shap...  30.5 us
    pallas_call x1, Pallas kernels, shards(): pl.pallas_call(output_kernel, out_shape=results, in_specs=[vmem] * 8, out...  2.67 us

profile of v5, /device:TPU:1, one launch (start us, length us, event | category | flops | bytes accessed | tf_op | source)
XLA Modules:
  0.0 33.8 jit_solution(13382264979376183965)
XLA Ops:
  0.6 30.5 %exchange.1 = (bf16[128,1024]{1,0:T(8,128)(2,1)S(1)}, bf16[128,1024]{1,0:T(8,128)(2,1)S(1)}, f32[3,128,1024]{2,1,0:T(8,128)S(1)}, bf16[3,128,128]{2,1,0:T(8,128)...) custom-call(bf16[3,2048]{1,0:T(4,128)(2,1)} %bitcast.7, ...), custom_call_target="tpu_custom_call" | custom-call | tf_op jit(solution)/shard_map/exchange/pallas_call | solution.py:370
  31.1 2.7 %outputs.1 = (f32[3,64,1024]{2,1,0:T(8,128)}, f32[3,1024]{1,0:T(4,128)}, f32[3,1024]{1,0:T(4,128)}, f32[1,1024]{1,0:T(1,128)}, f32[1024,1024]{1,0:T(8,128)}, /*index=5*/f32[1,1024]{1,0:T(1,128)}) custom-call(bf16[128,1024]{1,0:T(8,128)(2,1)S(1)} %get-tuple-element.20.hm, bf16[128,1024]{1,0:T(8,128)(2,1)S(1)} %get-tuple-element.21.prod, ...), custom_call_target="tpu_custom_call" | custom-call | tf_op jit(solution)/shard_map/outputs/pallas_call | solution.py:403
